TPU v7x, 128 devices: a whole 4x4x4 slice. The times are simulated.
128 devices in a mesh: gx: 4 (over z), gy: 32 (over y, x, core).
Axes of the slice: x: 4, y: 4, z: 4, core: 2. Of those that a mesh axis runs over, the one named last changes fastest.
Arguments:
- a_blocks: float32 [1024, 4, 128, 128], P(('gx', 'gy')), may hold values from -0.25 to 0.25
- a_cols: int32 [1024, 4], replicated, may hold values from 0 to 1023, as said below
- t_blocks: float32 [1024, 128, 128], P(('gx', 'gy')), may hold values from -0.5 to 0.5
- t_agg: int32 [1024], replicated, may hold values from 0 to 1, as said below
- dinv: float32 [1024, 128, 128], P(('gx', 'gy')), may hold values from -0.5 to 0.5
- coarse_inv: float32 [256, 128, 128], P(('gx', 'gy')), may hold values from -1.5 to 1.5
Outputs:
- coarse: float32 [256, 14, 128, 128], P(('gx', 'gy'))
Inputs may be any that keep to these rules, and one draw needn't show every extreme that they name: `a_cols`: block column 0 of row g is g itself; column 1 lies in g's own slab; column 2 lies in the slab below (on the cycle) and column 3 in the slab above; over the rows of one slab, columns 2 name exactly 4 distinct rows of the slab below, and columns 3 exactly 4 distinct rows of the slab above. `t_agg`: every slab's 2 aggregates each hold 4 of its rows.
All inputs are finite; a program needn't handle non-finite values.
Results may differ from a plain program's by a relative error of at most 0.0001.
Values sent between devices are 32-bit elements; how exact they have to be, the bound alone decides.
No kernel may reach another device: no remote copies, remote signals or barrier semaphores. Data moves between devices by JAX's collectives and lax.ppermute only.
A program may use at most 64 MiB of HBM per device.

v0:
```python
import functools

import jax
import jax.numpy as jnp
from jax import lax
from jax.experimental import pallas as pl
from jax.experimental.pallas import tpu as pltpu
from jax.sharding import PartitionSpec as P


OMEGA = 0.6
AXES = ("gx", "gy")
F32 = jnp.float32
BF16 = jnp.bfloat16
ROW, NEAR, POS2, POS3, LIST_0, OWN_LAB, SIDE_LAB, BACK, TAB = 0, 8, 16, 24, 32, 40, 72, 88, 96
LANES = 128
BELOW, ABOVE = 0, 1
ROW_CHUNK = 128


def exchanged(value, first):
    count = lax.axis_size(AXES)
    pairs = []
    for low in range(first, count + first, 2):
        high = (low + 1) % count
        pairs += [(low, high), (high, low)]
    return lax.ppermute(value, AXES, pairs)


def pair_side():
    return 1 - lax.rem(lax.axis_index("gy"), 2)


def split(x):
    high = x.astype(BF16)
    return high, (x - high.astype(F32)).astype(BF16)


def dot(a, b):
    return jnp.dot(a, b, preferred_element_type=F32)


def dot3(a_high, a_low, b_high, b_low):
    return dot(a_high, b_high) + dot(a_low, b_high) + dot(a_high, b_low)


def dot3k(a_high, a_low, b_high, b_low):
    both = jnp.concatenate([a_high, a_low], axis=1)
    return dot(both, jnp.concatenate([b_high, b_high], axis=0)) + dot(a_high, b_low)


def note(tab, i, value):
    tab[pl.ds(i, 1), :] = jnp.full((1, tab.shape[1]), value, jnp.int32)


def entry(tab, i):
    return tab[pl.ds(i, 1), :][0, 0]


def load_kernel(devices, cols_hbm, agg_hbm, t_hbm, tab, t_0, t_1, t, cols, agg, rank, sem):
    rows, width = t.shape[0], t.shape[0] // 2
    device = lax.axis_index("gx") * lax.axis_size("gy") + lax.axis_index("gy")
    previous = lax.rem(device + devices - 1, devices)
    following = lax.rem(device + 1, devices)
    slabs = previous, following, device
    side = pair_side()
    shift = ROW_CHUNK.bit_length() - 1
    chunk = 4 * ROW_CHUNK
    copies = [
        pltpu.make_async_copy(
            cols_hbm.at[pl.ds(pl.multiple_of(((slab * rows) >> shift) * chunk, chunk), chunk)],
            cols.at[pl.ds(i * chunk, chunk)],
            sem.at[i],
        )
        for i, slab in enumerate(slabs)
    ]
    copies += [pltpu.make_async_copy(t_hbm, t, sem.at[3]), pltpu.make_async_copy(agg_hbm, agg, sem.at[4])]
    for copy in copies:
        copy.start()

    def col(i, r, k):
        return cols[i * chunk + k * ROW_CHUNK + ((slabs[i] * rows) & (ROW_CHUNK - 1)) + r]

    def rank_rows(i, k, where):
        mask = jnp.int32(0)
        for r in range(rows):
            mask = mask | (jnp.int32(1) << (col(i, r, k) & (rows - 1)))
        named, other = jnp.int32(0), jnp.int32(width)
        for r in range(rows):
            hit = (mask >> r) & 1
            place = jnp.where(hit == 1, named, other)
            rank[where * rows + r] = place
            rank[(where + 1) * rows + place] = r
            named = named + hit
            other = other + 1 - hit

    def ranked(where, r):
        return rank[where * rows + r]

    copies[0].wait()
    copies[1].wait()
    rank_rows(0, 3, 0)
    rank_rows(1, 2, 2)
    sent_1, sent_0 = jnp.where(side == ABOVE, 0, 2), jnp.where(side == ABOVE, 2, 0)
    copies[3].wait()
    for j in range(width):
        t_1[j] = t[ranked(sent_1 + 1, j)]
        t_0[j] = t[ranked(sent_0 + 1, j)]
    copies[2].wait()
    copies[4].wait()
    rank_rows(2, 2, 4)
    rank_rows(2, 3, 6)
    for j in range(width):
        note(tab, LIST_0 + j, ranked(sent_1, ranked(sent_0 + 1, j)))
        for which in (BELOW, ABOVE):
            note(tab, BACK + width * which + j, col(which, ranked(5 + 2 * which, j), 3 - which) & (rows - 1))
            for k in range(2):
                note(tab, SIDE_LAB + 8 * which + 2 * j + k, agg[col(which, ranked(5 + 2 * which, j), 2 + k)])
    for u in range(rows):
        row = ranked(sent_1 + 1, u)
        note(tab, ROW + u, row)
        note(tab, NEAR + u, ranked(sent_1, col(2, row, 1) & (rows - 1)))
        note(tab, POS2 + u, ranked(4, col(2, row, 2) & (rows - 1)))
        note(tab, POS3 + u, ranked(6, col(2, row, 3) & (rows - 1)))
        for k in range(4):
            note(tab, OWN_LAB + 4 * u + k, agg[col(2, row, k)])


def put(value, label, column):
    return jnp.where(label == column, value, jnp.zeros_like(value))


def two_columns(value, label):
    return jnp.concatenate([put(value, label, 0), put(value, label, 1)], axis=1)


def near_tiles(tab, a, t, dinv, order):
    block = t.shape[1]
    rows = [entry(tab, ROW + u) for u in order]
    prods = []
    for u, row in zip(order, rows):
        near = entry(tab, ROW + entry(tab, NEAR + u))
        prods.append(
            jnp.concatenate(
                [dot3k(*split(a[row, 0]), *split(t[row])), dot3k(*split(a[row, 1]), *split(t[near]))], axis=1
            )
        )
    tiles = []
    for u, row, prod in zip(order, rows, prods):
        smoothed = dot3k(*split(dinv[row]), *split(prod))
        p0 = t[row] - OMEGA * smoothed[:, :block]
        p1 = -OMEGA * smoothed[:, block:]
        tiles.append(two_columns(p0, entry(tab, OWN_LAB + 4 * u)) + two_columns(p1, entry(tab, OWN_LAB + 4 * u + 1)))
    return tiles


def wide(ref, *places):
    return jnp.concatenate([ref[place] for place in places], axis=0)


def near_kernel(tab, a, t, dinv, near_0, near_1, own, a_high, a_low, a01_high, a01_low):
    rows, width = own.shape[0], near_1.shape[0]
    for u, value in enumerate(near_tiles(tab, a, t, dinv, range(rows))):
        own[u] = value
        if u < width:
            near_1[u] = value
    for j in range(width):
        near_0[j] = own[entry(tab, LIST_0 + j)]
    for u in range(rows):
        row = entry(tab, ROW + u)
        a01_high[u], a01_low[u] = split(jnp.concatenate([a[row, 0], a[row, 1]], axis=1))
        for which in (BELOW, ABOVE):
            a_high[which, u], a_low[which, u] = split(a[row, 2 + which])


def far_blocks(tab, a_high, a_low, dinv, t_high, t_low, order):
    prods = [
        jnp.concatenate(
            [
                dot3k(a_high[which, u], a_low[which, u], t_high[which, pos], t_low[which, pos])
                for which, pos in ((BELOW, entry(tab, POS2 + u)), (ABOVE, entry(tab, POS3 + u)))
            ],
            axis=1,
        )
        for u in order
    ]
    return [-OMEGA * dot3k(*split(dinv[entry(tab, ROW + u)]), *split(prod)) for u, prod in zip(order, prods)]


def split_rows(value, high, low):
    for j in range(value.shape[0]):
        high[j], low[j] = split(value[j])


def far_sent_kernel(tab, a_high, a_low, dinv, t_0, far_1, t_high, t_low):
    side = pair_side()
    block = dinv.shape[1]
    split_rows(t_0, t_high, t_low)
    order = range(far_1.shape[0])
    prods = []
    for u in order:
        pos = entry(tab, POS2 + 8 * side + u)
        high, low = split(dot3k(a_high[side, u], a_low[side, u], t_high[pos], t_low[pos]))
        prods.append(
            (jnp.concatenate([high, a_high[1 - side, u]], axis=1), jnp.concatenate([low, a_low[1 - side, u]], axis=1))
        )
    for u in order:
        both = -OMEGA * dot3k(*split(dinv[entry(tab, ROW + u)]), *prods[u])
        far_1[u, side] = both[:, :block]
        far_1[u, 1 - side] = both[:, block:]


def store_turned(trans, label, place, value):
    block = value.shape[0]
    trans[pl.ds(pl.multiple_of(label * block, block), block), place] = value.T
    trans[pl.ds(pl.multiple_of((1 - label) * block, block), block), place] = jnp.zeros_like(value)


def turn(tab, far, side, trans_high, trans_low):
    for u in range(far.shape[0]):
        block = far.shape[2]
        label = entry(tab, OWN_LAB + 4 * u + 2 + side)
        high, low = split(far[u, side])
        place = slice(u * block, (u + 1) * block)
        store_turned(trans_high, label, place, high)
        store_turned(trans_low, label, place, low)


def coarse_group(trans_high, trans_low, ap_high, ap_low):
    return dot3(trans_high[...], trans_low[...], ap_high[...], ap_low[...])


def mid_kernel(
    tab, a01_high, a01_low, a_high, a_low, dinv, t0_high, t0_low, t_1, far_1, near_0,
    far_0, far, trans_high, trans_low, part, ap_high, ap_low, group,
    t_high, t_low, far_high, far_low, p_high, p_low,
):
    rows, block = far.shape[0], far.shape[2]
    width = rows // 2
    side = pair_side()
    for j in range(width):
        t_high[side, j], t_low[side, j] = t0_high[j], t0_low[j]
        t_high[1 - side, j], t_low[1 - side, j] = split(t_1[j])
    for u in range(width):
        pos = entry(tab, POS2 + 8 * (1 - side) + u)
        far[u, side] = far_1[u, side]
        far[u, 1 - side] = dot3k(*split(far_1[u, 1 - side]), t_high[1 - side, pos], t_low[1 - side, pos])
    for u, both in enumerate(far_blocks(tab, a_high, a_low, dinv, t_high, t_low, range(width, rows))):
        far[width + u, BELOW] = both[:, :block]
        far[width + u, ABOVE] = both[:, block:]
    for j in range(width):
        far_0[j] = far[entry(tab, LIST_0 + j)]
        p_high[j], p_low[j] = split(near_0[j])
    for u in range(rows):
        for which in (BELOW, ABOVE):
            label = entry(tab, OWN_LAB + 4 * u + 2 + which)
            high, low = split(far[u, which])
            far_high[which, u] = two_columns(high, label)
            far_low[which, u] = two_columns(low, label)

    def mine(u, which):
        near = entry(tab, NEAR + u)
        return dot3(a01_high[u], a01_low[u], wide(far_high.at[which], u, near), wide(far_low.at[which], u, near))

    totals = []
    for u in range(rows):
        pos = entry(tab, POS2 + 8 * side + u)
        totals.append(mine(u, side) + dot3k(a_high[side, u], a_low[side, u], p_high[pos], p_low[pos]))
    for u in range(rows):
        place = slice(u * block, (u + 1) * block)
        ap_high[place], ap_low[place] = split(totals[u])
    turn(tab, far, 1 - side, trans_high, trans_low)
    for u in range(rows):
        part[u] = mine(u, 1 - side)
    group[...] = coarse_group(trans_high, trans_low, ap_high, ap_low)


def first_kernel(
    tab, a_high, a_low, part, trans_high, trans_low, near_1,
    ap_high, ap_low, out_1,
    p_high, p_low,
):
    rows, block = part.shape[0], part.shape[1]
    side = 1 - pair_side()
    split_rows(near_1, p_high, p_low)
    totals = []
    for u in range(rows):
        pos = entry(tab, POS2 + 8 * side + u)
        totals.append(part[u] + dot3k(a_high[side, u], a_low[side, u], p_high[pos], p_low[pos]))
    for u in range(rows):
        place = slice(u * block, (u + 1) * block)
        ap_high[place], ap_low[place] = split(totals[u])
    out_1[...] = coarse_group(trans_high, trans_low, ap_high, ap_low)


def far_columns(tab, side, a_high, a_low, p_high, p_low, ap_high, ap_low):
    rows, block = a_high.shape[1], a_high.shape[3]
    values, here = [], []
    for u in range(rows):
        pos = entry(tab, POS2 + 8 * side + u)
        values.append(dot3k(a_high[side, u], a_low[side, u], p_high[pos], p_low[pos]))
    for u in range(rows):
        labels = SIDE_LAB + 8 * side + 2 * entry(tab, POS2 + 8 * side + u)
        here.append(two_columns(values[u][:, :block], entry(tab, labels + 1 - side)))
        high, low = split(values[u][:, block:])
        label = entry(tab, labels + side)
        place = slice(u * block, (u + 1) * block)
        ap_high[place] = two_columns(high, label)
        ap_low[place] = two_columns(low, label)
    return here


def same_kernel(
    tab, a_high, a_low, trans_high, trans_low, far_0, group,
    own_part, ap_high, ap_low, out_1,
    p_high, p_low,
):
    half = trans_high.shape[0]
    block = half // 2
    side = pair_side()
    out_1[:, :half] = group[...]
    for j in range(far_0.shape[0]):
        p_high[j, :, :block], p_low[j, :, :block] = split(far_0[j, 1 - side])
        p_high[j, :, block:], p_low[j, :, block:] = split(far_0[j, side])
    here = far_columns(tab, side, a_high, a_low, p_high, p_low, ap_high, ap_low)
    for u, value in enumerate(here):
        own_part[u] = value
    out_1[:, half:] = coarse_group(trans_high, trans_low, ap_high, ap_low)


def own_part_kernel(tab, a01_high, a01_low, own, t, so_far, own_part, back_high, back_low, own_high, own_low):
    rows = own.shape[0]
    side = 1 - pair_side()
    for j in range(rows // 2):
        back_high[j], back_low[j] = split(t[entry(tab, BACK + (rows // 2) * side + j)])
    for u in range(rows):
        own_high[u], own_low[u] = split(own[u])
    for u in range(rows):
        near = entry(tab, NEAR + u)
        own_part[u] = so_far[u] + dot3(a01_high[u], a01_low[u], wide(own_high, u, near), wide(own_low, u, near))


def second_kernel(
    tab, a_high, a_low, own_part, back_high, back_low, trans_high, trans_low, far_1,
    own_high, own_low, ap_high, ap_low, out_1,
    p_high, p_low,
):
    rows, block = own_part.shape[0], own_part.shape[1]
    half = 2 * block
    side = 1 - pair_side()
    towards = [dot3k(*split(far_1[j, 1 - side]), back_high[j], back_low[j]) for j in range(rows // 2)]
    for j in range(rows // 2):
        p_high[j, :, :block], p_low[j, :, :block] = split(towards[j])
        p_high[j, :, block:], p_low[j, :, block:] = split(far_1[j, side])
    here = far_columns(tab, side, a_high, a_low, p_high, p_low, ap_high, ap_low)
    for u in range(rows):
        place = slice(u * block, (u + 1) * block)
        own_high[place], own_low[place] = split(own_part[u] + here[u])
    out_1[:, :half] = coarse_group(trans_high, trans_low, own_high, own_low)
    out_1[:, half:] = coarse_group(trans_high, trans_low, ap_high, ap_low)


def every_group(trans_high, trans_low, aps, out):
    half = trans_high.shape[0]
    for i in range(len(aps) // 2):
        out[:, i * half : (i + 1) * half] = coarse_group(trans_high, trans_low, aps[2 * i], aps[2 * i + 1])


def other_kernel(tab, far, *refs):
    aps, (out_0, trans_high, trans_low) = refs[:10], refs[10:]
    turn(tab, far, pair_side(), trans_high, trans_low)
    every_group(trans_high, trans_low, aps, out_0)


def own_kernel(own, *refs):
    aps, (out, trans_high, trans_low) = refs[:10], refs[10:]
    rows, block = own.shape[0], own.shape[1]
    for u in range(rows):
        place = slice(u * block, (u + 1) * block)
        high, low = split(own[u])
        trans_high[:, place] = high.T
        trans_low[:, place] = low.T
    every_group(trans_high, trans_low, aps, out)


def write_slots(inverse, totals, results, out, sems):
    block = inverse.shape[1]
    inv = [split(inverse[agg]) for agg in range(2)]
    values = [dot3k(*inv[agg], *split(total)) for agg, _, total in totals]
    copies = []
    for n, ((agg, d, _), value) in enumerate(zip(totals, values)):
        results[n, 0] = value[:, :block]
        results[n, 1] = value[:, block:]
        copies.append(pltpu.make_async_copy(results.at[n], out.at[agg, pl.ds(2 * (d + 3), 2)], sems.at[n]))
        copies[-1].start()
    for copy in copies:
        copy.wait()


OWN_AT, SAME_AT = (1, -1, 2, 0, -2), (0, 2, -1, 1, 3)
PARTS_AT = (-2, -3), (-1, 1), (0,)


def finish_kernel(offsets, part_at, inverse, own, both_0, part, *refs):
    out, results, sems = refs[-3:]
    block = inverse.shape[1]
    half = 2 * block
    side = pair_side()

    def run(way):
        done = []
        for agg in range(2):
            line = slice(agg * block, (agg + 1) * block)
            for d in offsets:
                places = [(ref, at.index(d)) for ref, at in ((own, OWN_AT), (both_0, SAME_AT), (part, part_at)) if d in at]
                shares = [ref[line, i * half : (i + 1) * half] for ref, i in places]
                done.append((agg, way * d, sum(shares[1:], shares[0])))
        write_slots(inverse, done, results, out, sems)

    pl.when(side == ABOVE)(lambda: run(1))
    pl.when(side == BELOW)(lambda: run(-1))


VMEM = pl.BlockSpec(memory_space=pltpu.VMEM)
HBM = pl.BlockSpec(memory_space=pltpu.HBM)


def call(body, outs, ins, scratch=(), micros=1.0, in_hbm=(), out_hbm=(), aliases={}):
    def specs(values, in_place):
        return [HBM if i in in_place else VMEM for i, x in enumerate(values)]

    return pl.pallas_call(
        body,
        out_shape=outs,
        in_specs=specs(ins, in_hbm),
        out_specs=specs(outs, out_hbm),
        scratch_shapes=[pltpu.VMEM(*x) if isinstance(x, tuple) else x for x in scratch],
        input_output_aliases=aliases,
        compiler_params=pltpu.CompilerParams(vmem_limit_bytes=24 * 2**20),
        cost_estimate=pl.CostEstimate(flops=int(micros * 1e9), bytes_accessed=2**20, transcendentals=0),
    )(*ins)


def shards(a, a_cols, t_blocks, t_agg, dinv, coarse_inv):
    devices = lax.axis_size(AXES)
    rows, block = t_blocks.shape[:2]
    width, half, deep = rows // 2, 2 * block, rows * block
    shape = jax.ShapeDtypeStruct
    full = lambda *dims: shape(dims, F32)
    pair = lambda *dims: [shape(dims, BF16), shape(dims, BF16)]
    two = lambda *dims: [(dims, BF16)] * 2
    tile = full(width, block, half)
    cols = a_cols.reshape(-1, ROW_CHUNK, 4).transpose(0, 2, 1).reshape(-1)

    tab, t_0, t_1, t = call(
        functools.partial(load_kernel, devices),
        [shape((TAB, LANES), jnp.int32)] + [full(width, block, block)] * 2 + [full(*t_blocks.shape)],
        [pltpu.with_memory_space_constraint(x, pltpu.HBM) for x in (cols, t_agg, t_blocks)],
        [
            pltpu.SMEM((3 * 4 * ROW_CHUNK,), jnp.int32),
            pltpu.SMEM(t_agg.shape, jnp.int32),
            pltpu.SMEM((8 * rows,), jnp.int32),
            pltpu.SemaphoreType.DMA((5,)),
        ],
        micros=3,
        in_hbm=(0, 1, 2),
    )
    t_1 = exchanged(t_1, 1)
    t_0 = exchanged(t_0, 0)
    near_0, near_1, own, a23_high, a23_low, a01_high, a01_low = call(
        near_kernel,
        [tile, tile, full(rows, block, half)] + pair(2, rows, block, block) + pair(rows, block, half),
        [tab, a, t, dinv],
        micros=2,
    )
    near_0 = exchanged(near_0, 0)
    sent = full(width, 2, block, block)
    far_1, t0_high, t0_low = call(
        far_sent_kernel, [sent] + pair(width, block, block), [tab, a23_high, a23_low, dinv, t_0], micros=2
    )
    got_far_1 = exchanged(far_1, 1)
    far_0, far, out_high, out_low, part, ap_e1_high, ap_e1_low, group = call(
        mid_kernel,
        [sent, full(rows, 2, block, block)]
        + pair(half, deep)
        + [full(rows, block, half)]
        + pair(deep, half)
        + [full(half, half)],
        [tab, a01_high, a01_low, a23_high, a23_low, dinv, t0_high, t0_low, t_1, far_1, near_0],
        two(2, width, block, block) + two(2, rows, block, half) + two(width, block, half),
        micros=3,
    )
    near_1 = exchanged(near_1, 1)
    far_0, far_1 = exchanged(far_0, 0), got_far_1
    part_own, ap_e2_high, ap_e2_low, part_1 = call(
        same_kernel,
        [full(rows, block, half)] + pair(deep, half) + [full(half, 2 * half)],
        [tab, a23_high, a23_low, out_high, out_low, far_0, group],
        two(width, block, half),
        micros=1,
    )
    part_1 = exchanged(part_1, 1)
    part_own, back_high, back_low = call(
        own_part_kernel,
        [full(rows, block, half)] + pair(width, block, block),
        [tab, a01_high, a01_low, own, t, part_own],
        two(rows, block, half),
        micros=1,
    )
    ap_own_high, ap_own_low, ap_o2_high, ap_o2_low, part_2 = call(
        second_kernel,
        pair(deep, half) * 2 + [full(half, 2 * half)],
        [tab, a23_high, a23_low, part_own, back_high, back_low, out_high, out_low, far_1],
        two(width, block, half),
        micros=2,
    )
    part_2 = exchanged(part_2, 1)
    ap_o1_high, ap_o1_low, part_3 = call(
        first_kernel,
        pair(deep, half) + [full(half, half)],
        [tab, a23_high, a23_low, part, out_high, out_low, near_1],
        two(width, block, half),
        micros=2,
    )
    part_3 = exchanged(part_3, 1)
    aps = [
        ap_e1_high, ap_e1_low, ap_o1_high, ap_o1_low, ap_e2_high, ap_e2_low,
        ap_own_high, ap_own_low, ap_o2_high, ap_o2_low,
    ]
    (both_0,) = call(other_kernel, [full(half, 5 * half)], [tab, far] + aps, two(half, deep), micros=2)
    both_0 = exchanged(both_0, 0)
    (total,) = call(own_kernel, [full(half, 5 * half)], [own] + aps, two(half, deep), micros=2)
    out = []
    for i, (offsets, got) in enumerate((((-3, -2, 2, 3), part_1), ((-1, 1), part_2), ((0,), part_3))):
        n = 2 * len(offsets)
        out = call(
            functools.partial(finish_kernel, offsets, PARTS_AT[i]),
            [full(2, 14, block, block)],
            [coarse_inv, total, both_0, got, *out],
            [((n, 2, block, block), F32), pltpu.SemaphoreType.DMA((n,))],
            micros=1,
            in_hbm=(4,),
            out_hbm=(0,),
            aliases={4: 0} if i else {},
        )
    return out[0]


def solution(mesh):
    placed = (
        P(AXES, None, None, None),
        P(),
        P(AXES, None, None),
        P(),
        P(AXES, None, None),
        P(AXES, None, None),
    )
    return jax.shard_map(
        shards,
        mesh=mesh,
        in_specs=placed,
        out_specs=P(AXES, None, None, None),
        check_vma=False,
    )
```

profile of v0, /device:TPU:0, one launch (start us, length us, event | category | flops | bytes accessed | tf_op | source)
XLA Modules:
  0.0 63.0 jit_solution(14444818413349914103)
XLA Ops:
  0.0 1.5 %shard_map.64 = (s32[96,128]{1,0:T(8,128)S(1)}, f32[4,128,128]{2,1,0:T(8,128)S(1)}, f32[4,128,128]{2,1,0:T(8,128)S(1)}, f32[8,128,128]{2,1,0:T(8,128)S(1)}) custom-call(s32[4096]{0:T(1024)} %bitcast.5, s32[1024]{0:T(1024)} %agg_hbm.1, f32[8,128,128]{2,1,0:T(8,128)} %t_hbm.1), custom_call_target="tpu_custom_call" | custom-call | flops 3000000000 | bytes 1048576 | tf_op jit(solution)/shard_map/pallas_call | solution.py:432
  1.5 0.3 copy-done.1
  1.7 0.1 copy-done.2
  1.8 1.2 %shard_map.65 = (f32[4,128,256]{2,1,0:T(8,128)S(1)}, f32[4,128,256]{2,1,0:T(8,128)S(1)}, f32[8,128,256]{2,1,0:T(8,128)S(1)}, bf16[2,8,128,128]{3,2,1,0:T(8,128)(...) custom-call(s32[96,128]{1,0:T(8,128)S(1)} %get-tuple-element.42.tab,, ...), custom_call_target="tpu_custom_call" | custom-call | flops 2000000000 | bytes 1048576 | tf_op jit(solution)/shard_map/pallas_call | solution.py:432
  3.1 0.1 collective-permute-start.2
  3.2 0.5 collective-permute-start
  3.7 8.5 %collective-permute-start.1 = (f32[4,128,128]{2,1,0:T(8,128)S(1)}, f32[4,128,128]{2,1,0:T(8,128)S(1)}, u32[]{:S(2)}, u32[]{:S(2)}) collective-permute-start(f32[4,128,128]{2,1,0:T(8,128)S(1)} %get-tuple-element.52), channel_id=1, source_target_pairs={{1,2},{2,1},{3,4},{4,3},{5,6},{6,5},{7,8},{8,7},{9,10},{10,9},{11,... | collective-permute-start | bytes 786440 | tf_op jit(solution)/shard_map/ppermute | solution.py:27
  12.2 0.0 collective-permute-start.3
  12.2 0.0 collective-permute-done.t_0
  12.2 0.5 shard_map.66
  12.7 3.5 %collective-permute-done.1.t_1 = f32[4,128,128]{2,1,0:T(8,128)S(1)} collective-permute-done((f32[4,128,128]{2,1,0:T(8,128)S(1)}, f32[4,128,128]{2,1,0:T(8,128)S(1)}, u32[]{:S(2)}, u32[]{:S(2)}) %collective-permute-start.1) | collective-permute-done | bytes 262176 | tf_op jit(solution)/shard_map/ppermute | solution.py:27
  16.2 0.0 collective-permute-done.2.near_0
  16.2 2.8 %shard_map.67 = (f32[4,2,128,128]{3,2,1,0:T(8,128)S(1)}, f32[8,2,128,128]{3,2,1,0:T(8,128)S(1)}, bf16[256,1024]{1,0:T(8,128)(2,1)S(1)}, bf16[256,1024]{1,0:T(8,1...) custom-call(s32[96,128]{1,0:T(8,128)S(1)} %get-tuple-element.42.tab,, ...), custom_call_target="tpu_custom_call" | custom-call | flops 3000000000 | bytes 1048576 | tf_op jit(solution)/shard_map/pallas_call | solution.py:432
  19.1 0.1 collective-permute-start.4
  19.2 7.2 %collective-permute-start.5 = (f32[4,2,128,128]{3,2,1,0:T(8,128)S(1)}, f32[4,2,128,128]{3,2,1,0:T(8,128)S(1)}, u32[]{:S(2)}, u32[]{:S(2)}) collective-permute-start(f32[4,2,128,128]{3,2,1,0:T(8,128)S(1)} %get-tuple-element.53.far_1), channel_id=1, source_target_pairs={{1,2},{2,1},{3,4},{4,3},{5,6},{6,5},{7,8},{8,7},{9,10},{10,9},{11,... | collective-permute-start | bytes 1572872 | tf_op jit(solution)/shard_map/ppermute | solution.py:27
  26.4 1.0 %shard_map.68 = (bf16[1024,256]{1,0:T(8,128)(2,1)S(1)}, bf16[1024,256]{1,0:T(8,128)(2,1)S(1)}, f32[256,256]{1,0:T(8,128)S(1)}) custom-call(s32[96,128]{1,0:T(8,128)S(1)} %get-tuple-element.42.tab, bf16[2,8,128,128]{3,2,1,0:T(8,128)(2,1)S(1)} %get-tuple-element.47.a_high, bf16[2,8,128,128]{3,2,1,0:T(8,128)(2,1)S(1)} %get-tuple-element.48.a_low, ...), custom_call_target="tpu_custom_call" | custom-call | flops 2000000000 | bytes 1048576 | tf_op jit(solution)/shard_map/pallas_call | solution.py:432
  27.4 1.1 %shard_map.69 = (f32[8,128,256]{2,1,0:T(8,128)S(1)}, bf16[1024,256]{1,0:T(8,128)(2,1)S(1)}, bf16[1024,256]{1,0:T(8,128)(2,1)S(1)}, f32[256,512]{1,0:T(8,128)S(1)}) custom-call(s32[96,128]{1,0:T(8,128)S(1)} %get-tuple-element.42.tab, bf16[2,8,128,128]{3,2,1,0:T(8,128)(2,1)S(1)} %get-tuple-element.47.a_high, ...), custom_call_target="tpu_custom_call" | custom-call | flops 1000000000 | bytes 1048576 | tf_op jit(solution)/shard_map/pallas_call | solution.py:432
  28.5 0.8 %shard_map.70 = (f32[8,128,256]{2,1,0:T(8,128)S(1)}, bf16[4,128,128]{2,1,0:T(8,128)(2,1)S(1)}, bf16[4,128,128]{2,1,0:T(8,128)(2,1)S(1)}) custom-call(s32[96,128]{1,0:T(8,128)S(1)} %get-tuple-element.42.tab, bf16[8,128,256]{2,1,0:T(8,128)(2,1)S(1)} %get-tuple-element.45.a01_high, bf16[8,128,256]{2,1,0:T(8,128)(2,1)S(1)} %get-tuple-element.46.a01_low, ...), custom_call_target="tpu_custom_call" | custom-call | flops 1000000000 | bytes 1048576 | tf_op jit(solution)/shard_map/pallas_call | solution.py:432
  29.3 4.0 %collective-permute-done.5.far_1 = f32[4,2,128,128]{3,2,1,0:T(8,128)S(1)} collective-permute-done((f32[4,2,128,128]{3,2,1,0:T(8,128)S(1)}, f32[4,2,128,128]{3,2,1,0:T(8,128)S(1)}, u32[]{:S(2)}, u32[]{:S(2)}) %collective-permute-start.5) | collective-permute-done | bytes 524320 | tf_op jit(solution)/shard_map/ppermute | solution.py:27
  33.3 1.7 %shard_map.71 = (bf16[1024,256]{1,0:T(8,128)(2,1)S(1)}, bf16[1024,256]{1,0:T(8,128)(2,1)S(1)}, bf16[1024,256]{1,0:T(8,128)(2,1)S(1)}, bf16[1024,256]{1,0:T(8,128)(2,1)S(1)}, f32[256,512]{1,0:T(8,128)S(1)}) custom-call(s32[96,128]{1,0:T(8,128)S(1)} %get-tuple-element.42.tab, bf16[2,8,128,128]{3,2,1,0:T(8,128)(2,1)S(1)} %get-tuple-element.47.a_high, ...), custom_call_target="tpu_custom_call" | custom-call | flops 2000000000 | bytes 1048576 | tf_op jit(solution)/shard_map/pallas_call | solution.py:432
  35.0 2.5 %shard_map.73 = f32[256,1280]{1,0:T(8,128)S(1)} custom-call(s32[96,128]{1,0:T(8,128)S(1)} %get-tuple-element.42.tab, f32[8,2,128,128]{3,2,1,0:T(8,128)S(1)} %get-tuple-element.75.far, bf16[1024,256]{1,0:T(8,128)(2,1)S(1)} %get-tuple-element.55.refs_0_, bf16[1024,256]{1,0:T(8,128)(2,1)S(1)} %get-tuple-element.56.refs_1_, ...), custom_call_target="tpu_custom_call" | custom-call | flops 2000000000 | bytes 1048576 | tf_op jit(solution)/shard_map/pallas_call | solution.py:432
  37.5 0.3 collective-permute-start.6
  37.7 7.3 %collective-permute-start.9 = (f32[256,512]{1,0:T(8,128)S(1)}, f32[256,512]{1,0:T(8,128)S(1)}, u32[]{:S(2)}, u32[]{:S(2)}) collective-permute-start(f32[256,512]{1,0:T(8,128)S(1)} %get-tuple-element.78), channel_id=1, source_target_pairs={{1,2},{2,1},{3,4},{4,3},{5,6},{6,5},{7,8},{8,7},{9,10},{10,9},{11,... | collective-permute-start | bytes 1572872 | tf_op jit(solution)/shard_map/ppermute | solution.py:27
  45.0 0.1 collective-permute-start.8
  45.1 7.1 %collective-permute-start.7 = (f32[256,256]{1,0:T(8,128)S(1)}, f32[256,256]{1,0:T(8,128)S(1)}, u32[]{:S(2)}, u32[]{:S(2)}) collective-permute-start(f32[256,256]{1,0:T(8,128)S(1)} %get-tuple-element.76), channel_id=1, source_target_pairs={{1,2},{2,1},{3,4},{4,3},{5,6},{6,5},{7,8},{8,7},{9,10},{10,9},{11,... | collective-permute-start | bytes 786440 | tf_op jit(solution)/shard_map/ppermute | solution.py:27
  52.2 2.3 %shard_map.72.own = f32[256,1280]{1,0:T(8,128)S(1)} custom-call(f32[8,128,256]{2,1,0:T(8,128)S(1)} %get-tuple-element.44.own, bf16[1024,256]{1,0:T(8,128)(2,1)S(1)} %get-tuple-element.55.refs_0_, bf16[1024,256]{1,0:T(8,128)(2,1)S(1)} %get-tuple-element.56.refs_1_, bf16[1024,256]{1,0:T(8,128)(2,1)S(1)} %get-tuple-element.61.refs_2_, ...), custom_call_target="tpu_custom_call" | custom-call | flops 2000000000 | bytes 1048576 | tf_op jit(solution)/shard_map/pallas_call | solution.py:432
  54.5 0.0 collective-permute-done.9.part
  54.5 1.3 %shard_map.74.refs_0_ = f32[2,14,128,128]{3,2,1,0:T(8,128)} custom-call(f32[2,128,128]{2,1,0:T(8,128)S(1)} %copy-done, f32[256,1280]{1,0:T(8,128)S(1)} %shard_map.72.own, f32[256,1280]{1,0:T(8,128)S(1)} %collective-permute-done.6.both_0, f32[256,512]{1,0:T(8,128)S(1)} %collective-permute-done.9.part), custom_call_target="tpu_custom_call" | custom-call | flops 1000000000 | bytes 1048576 | tf_op jit(solution)/shard_map/pallas_call | solution.py:432
  55.8 3.3 %collective-permute-done.8.part = f32[256,512]{1,0:T(8,128)S(1)} collective-permute-done((f32[256,512]{1,0:T(8,128)S(1)}, f32[256,512]{1,0:T(8,128)S(1)}, u32[]{:S(2)}, u32[]{:S(2)}) %collective-permute-start.8) | collective-permute-done | bytes 524320 | tf_op jit(solution)/shard_map/ppermute | solution.py:27
  59.0 1.1 %shard_map.75.refs_0_ = f32[2,14,128,128]{3,2,1,0:T(8,128)} custom-call(f32[2,128,128]{2,1,0:T(8,128)S(1)} %copy-done, f32[256,1280]{1,0:T(8,128)S(1)} %shard_map.72.own, f32[256,1280]{1,0:T(8,128)S(1)} %collective-permute-done.6.both_0, f32[256,512]{1,0:T(8,128)S(1)} %collective-permute-done.8.part, ...), custom_call_target="tpu_custom_call", output_to_operand_aliasing={{}: (4, {})} | custom-call | flops 1000000000 | bytes 1048576 | tf_op jit(solution)/shard_map/pallas_call | solution.py:432
  60.1 1.7 %collective-permute-done.7.part = f32[256,256]{1,0:T(8,128)S(1)} collective-permute-done((f32[256,256]{1,0:T(8,128)S(1)}, f32[256,256]{1,0:T(8,128)S(1)}, u32[]{:S(2)}, u32[]{:S(2)}) %collective-permute-start.7) | collective-permute-done | bytes 262176 | tf_op jit(solution)/shard_map/ppermute | solution.py:27
  61.8 1.0 %shard_map.76 = f32[2,14,128,128]{3,2,1,0:T(8,128)} custom-call(f32[2,128,128]{2,1,0:T(8,128)S(1)} %copy-done, f32[256,1280]{1,0:T(8,128)S(1)} %shard_map.72.own, f32[256,1280]{1,0:T(8,128)S(1)} %collective-permute-done.6.both_0, f32[256,256]{1,0:T(8,128)S(1)} %collective-permute-done.7.part, ...), custom_call_target="tpu_custom_call", output_to_operand_aliasing={{}: (4, {})} | custom-call | flops 1000000000 | bytes 1048576 | tf_op jit(solution)/shard_map/pallas_call | solution.py:432
  (7 shorter events, 0.0 us)
Async XLA Ops:
  0.0 1.7 %copy-start.1 = (f32[8,4,128,128]{3,2,1,0:T(8,128)S(1)}, f32[8,4,128,128]{3,2,1,0:T(8,128)}, u32[]{:S(2)}) copy-start(f32[8,4,128,128]{3,2,1,0:T(8,128)} %a.1) | copy-start | bytes 6291460
  0.0 1.8 %copy-start.2 = (f32[8,128,128]{2,1,0:T(8,128)S(1)}, f32[8,128,128]{2,1,0:T(8,128)}, u32[]{:S(2)}) copy-start(f32[8,128,128]{2,1,0:T(8,128)} %dinv.5) | copy-start | bytes 1572868
  3.1 13.1 %collective-permute-start.2 = (f32[4,128,256]{2,1,0:T(8,128)S(1)}, f32[4,128,256]{2,1,0:T(8,128)S(1)}, u32[]{:S(2)}, u32[]{:S(2)}) collective-permute-start(f32[4,128,256]{2,1,0:T(8,128)S(1)} %get-tuple-element.54), channel_id=1, source_target_pairs={{0,1},{1,0},{2,3},{3,2},{4,5},{5,4},{6,7},{7,6},{8,9},{9,8},{10,11... | collective-permute-start | bytes 1572872 | tf_op jit(solution)/shard_map/ppermute | solution.py:27
  3.2 9.0 %collective-permute-start = (f32[4,128,128]{2,1,0:T(8,128)S(1)}, f32[4,128,128]{2,1,0:T(8,128)S(1)}, u32[]{:S(2)}, u32[]{:S(2)}) collective-permute-start(f32[4,128,128]{2,1,0:T(8,128)S(1)} %get-tuple-element.49), channel_id=1, source_target_pairs={{0,1},{1,0},{2,3},{3,2},{4,5},{5,4},{6,7},{7,6},{8,9},{9,8},{10,11... | collective-permute-start | bytes 786440 | tf_op jit(solution)/shard_map/ppermute | solution.py:27
  3.7 12.6 %collective-permute-start.1 = (f32[4,128,128]{2,1,0:T(8,128)S(1)}, f32[4,128,128]{2,1,0:T(8,128)S(1)}, u32[]{:S(2)}, u32[]{:S(2)}) collective-permute-start(f32[4,128,128]{2,1,0:T(8,128)S(1)} %get-tuple-element.52), channel_id=1, source_target_pairs={{1,2},{2,1},{3,4},{4,3},{5,6},{6,5},{7,8},{8,7},{9,10},{10,9},{11,... | collective-permute-start | bytes 786440 | tf_op jit(solution)/shard_map/ppermute | solution.py:27
  12.2 14.2 %collective-permute-start.3 = (f32[4,128,256]{2,1,0:T(8,128)S(1)}, f32[4,128,256]{2,1,0:T(8,128)S(1)}, u32[]{:S(2)}, u32[]{:S(2)}) collective-permute-start(f32[4,128,256]{2,1,0:T(8,128)S(1)} %get-tuple-element.60), channel_id=1, source_target_pairs={{1,2},{2,1},{3,4},{4,3},{5,6},{6,5},{7,8},{8,7},{9,10},{10,9},{11,... | collective-permute-start | bytes 1572872 | tf_op jit(solution)/shard_map/ppermute | solution.py:27
  19.1 8.4 %collective-permute-start.4 = (f32[4,2,128,128]{3,2,1,0:T(8,128)S(1)}, f32[4,2,128,128]{3,2,1,0:T(8,128)S(1)}, u32[]{:S(2)}, u32[]{:S(2)}) collective-permute-start(f32[4,2,128,128]{3,2,1,0:T(8,128)S(1)} %get-tuple-element.63), channel_id=1, source_target_pairs={{0,1},{1,0},{2,3},{3,2},{4,5},{5,4},{6,7},{7,6},{8,9},{9,8},{10,11... | collective-permute-start | bytes 1572872 | tf_op jit(solution)/shard_map/ppermute | solution.py:27
  19.2 14.1 %collective-permute-start.5 = (f32[4,2,128,128]{3,2,1,0:T(8,128)S(1)}, f32[4,2,128,128]{3,2,1,0:T(8,128)S(1)}, u32[]{:S(2)}, u32[]{:S(2)}) collective-permute-start(f32[4,2,128,128]{3,2,1,0:T(8,128)S(1)} %get-tuple-element.53.far_1), channel_id=1, source_target_pairs={{1,2},{2,1},{3,4},{4,3},{5,6},{6,5},{7,8},{8,7},{9,10},{10,9},{11,... | collective-permute-start | bytes 1572872 | tf_op jit(solution)/shard_map/ppermute | solution.py:27
  37.5 17.0 %collective-permute-start.6 = (f32[256,1280]{1,0:T(8,128)S(1)}, f32[256,1280]{1,0:T(8,128)S(1)}, u32[]{:S(2)}, u32[]{:S(2)}) collective-permute-start(f32[256,1280]{1,0:T(8,128)S(1)} %shard_map.73), channel_id=1, source_target_pairs={{0,1},{1,0},{2,3},{3,2},{4,5},{5,4},{6,7},{7,6},{8,9},{9,8},{10,11... | collective-permute-start | bytes 3932168 | tf_op jit(solution)/shard_map/ppermute | solution.py:27
  37.7 16.7 %collective-permute-start.9 = (f32[256,512]{1,0:T(8,128)S(1)}, f32[256,512]{1,0:T(8,128)S(1)}, u32[]{:S(2)}, u32[]{:S(2)}) collective-permute-start(f32[256,512]{1,0:T(8,128)S(1)} %get-tuple-element.78), channel_id=1, source_target_pairs={{1,2},{2,1},{3,4},{4,3},{5,6},{6,5},{7,8},{8,7},{9,10},{10,9},{11,... | collective-permute-start | bytes 1572872 | tf_op jit(solution)/shard_map/ppermute | solution.py:27
  45.0 14.0 %collective-permute-start.8 = (f32[256,512]{1,0:T(8,128)S(1)}, f32[256,512]{1,0:T(8,128)S(1)}, u32[]{:S(2)}, u32[]{:S(2)}) collective-permute-start(f32[256,512]{1,0:T(8,128)S(1)} %get-tuple-element.77), channel_id=1, source_target_pairs={{1,2},{2,1},{3,4},{4,3},{5,6},{6,5},{7,8},{8,7},{9,10},{10,9},{11,... | collective-permute-start | bytes 1572872 | tf_op jit(solution)/shard_map/ppermute | solution.py:27
  45.1 9.4 %copy-start = (f32[2,128,128]{2,1,0:T(8,128)S(1)}, f32[2,128,128]{2,1,0:T(8,128)}, u32[]{:S(2)}) copy-start(f32[2,128,128]{2,1,0:T(8,128)} %inverse.5) | copy-start | bytes 393220
  45.1 16.7 %collective-permute-start.7 = (f32[256,256]{1,0:T(8,128)S(1)}, f32[256,256]{1,0:T(8,128)S(1)}, u32[]{:S(2)}, u32[]{:S(2)}) collective-permute-start(f32[256,256]{1,0:T(8,128)S(1)} %get-tuple-element.76), channel_id=1, source_target_pairs={{1,2},{2,1},{3,4},{4,3},{5,6},{6,5},{7,8},{8,7},{9,10},{10,9},{11,... | collective-permute-start | bytes 786440 | tf_op jit(solution)/shard_map/ppermute | solution.py:27
where the time goes:
time: 63.1 us; the launch traced here: 63 us
  starting transfers between devices  31.1 us (49%)
  Pallas kernels  18.7 us (30%)
  waiting for transfers between devices  12.5 us (20%)
    ppermute x10, starting transfers between devices, exchanged(): return lax.ppermute(value, AXES, pairs)  31.1 us
    pallas_call x13, Pallas kernels, call(): pl.pallas_call(body, out_shape=outs, in_specs=specs(ins, in_hbm), out_spe...  18.7 us
    ppermute x10, waiting for transfers between devices, exchanged(): return lax.ppermute(value, AXES, pairs)  12.5 us
  transfers between devices with their start and end apart: 10, of which 4 were waited for; matrix products, arithmetic and copies ran while one was open for 0% of the time, Pallas kernels for 17%

commit v1 on v0

--- a/solution.py
+++ b/solution.py
@@ -230,11 +230,7 @@
     return dot3(trans_high[...], trans_low[...], ap_high[...], ap_low[...])
 
 
-def mid_kernel(
-    tab, a01_high, a01_low, a_high, a_low, dinv, t0_high, t0_low, t_1, far_1, near_0,
-    far_0, far, trans_high, trans_low, part, ap_high, ap_low, group,
-    t_high, t_low, far_high, far_low, p_high, p_low,
-):
+def far_kernel(tab, a_high, a_low, dinv, t0_high, t0_low, t_1, far_1, after, far_0, far, t_high, t_low):
     rows, block = far.shape[0], far.shape[2]
     width = rows // 2
     side = pair_side()
@@ -250,7 +246,16 @@
         far[width + u, ABOVE] = both[:, block:]
     for j in range(width):
         far_0[j] = far[entry(tab, LIST_0 + j)]
-        p_high[j], p_low[j] = split(near_0[j])
+
+
+def mid_kernel(
+    tab, a01_high, a01_low, a_high, a_low, far, near_0,
+    trans_high, trans_low, part, ap_high, ap_low, group,
+    far_high, far_low, p_high, p_low,
+):
+    rows, block = far.shape[0], far.shape[2]
+    side = pair_side()
+    split_rows(near_0, p_high, p_low)
     for u in range(rows):
         for which in (BELOW, ABOVE):
             label = entry(tab, OWN_LAB + 4 * u + 2 + which)
@@ -311,7 +316,7 @@
 
 
 def same_kernel(
-    tab, a_high, a_low, trans_high, trans_low, far_0, group,
+    tab, a_high, a_low, trans_high, trans_low, far_0, group, so_far,
     own_part, ap_high, ap_low, out_1,
     p_high, p_low,
 ):
@@ -324,11 +329,11 @@
         p_high[j, :, block:], p_low[j, :, block:] = split(far_0[j, side])
     here = far_columns(tab, side, a_high, a_low, p_high, p_low, ap_high, ap_low)
     for u, value in enumerate(here):
-        own_part[u] = value
+        own_part[u] = so_far[u] + value
     out_1[:, half:] = coarse_group(trans_high, trans_low, ap_high, ap_low)
 
 
-def own_part_kernel(tab, a01_high, a01_low, own, t, so_far, own_part, back_high, back_low, own_high, own_low):
+def own_part_kernel(tab, a01_high, a01_low, own, t, own_part, back_high, back_low, own_high, own_low):
     rows = own.shape[0]
     side = 1 - pair_side()
     for j in range(rows // 2):
@@ -337,7 +342,7 @@
         own_high[u], own_low[u] = split(own[u])
     for u in range(rows):
         near = entry(tab, NEAR + u)
-        own_part[u] = so_far[u] + dot3(a01_high[u], a01_low[u], wide(own_high, u, near), wide(own_low, u, near))
+        own_part[u] = dot3(a01_high[u], a01_low[u], wide(own_high, u, near), wide(own_low, u, near))
 
 
 def second_kernel(
@@ -401,8 +406,9 @@
 PARTS_AT = (-2, -3), (-1, 1), (0,)
 
 
-def finish_kernel(offsets, part_at, inverse, own, both_0, part, *refs):
-    out, results, sems = refs[-3:]
+def finish_kernel(offsets, part_at, inverse, own, *refs):
+    refs, (out, results, sems) = refs[:-3], refs[-3:]
+    others = ((refs[0], SAME_AT), (refs[1], part_at)) if len(refs) > 1 else ((refs[0], part_at),)
     block = inverse.shape[1]
     half = 2 * block
     side = pair_side()
@@ -412,7 +418,7 @@
         for agg in range(2):
             line = slice(agg * block, (agg + 1) * block)
             for d in offsets:
-                places = [(ref, at.index(d)) for ref, at in ((own, OWN_AT), (both_0, SAME_AT), (part, part_at)) if d in at]
+                places = [(ref, at.index(d)) for ref, at in ((own, OWN_AT), *others) if d in at]
                 shares = [ref[line, i * half : (i + 1) * half] for ref, i in places]
                 done.append((agg, way * d, sum(shares[1:], shares[0])))
         write_slots(inverse, done, results, out, sems)
@@ -479,34 +485,37 @@
         far_sent_kernel, [sent] + pair(width, block, block), [tab, a23_high, a23_low, dinv, t_0], micros=2
     )
     got_far_1 = exchanged(far_1, 1)
-    far_0, far, out_high, out_low, part, ap_e1_high, ap_e1_low, group = call(
+    near_1 = exchanged(near_1, 1)
+    part_own, back_high, back_low = call(
+        own_part_kernel,
+        [full(rows, block, half)] + pair(width, block, block),
+        [tab, a01_high, a01_low, own, t],
+        two(rows, block, half),
+        micros=1,
+    )
+    far_0, far = call(
+        far_kernel,
+        [sent, full(rows, 2, block, block)],
+        [tab, a23_high, a23_low, dinv, t0_high, t0_low, t_1, far_1, part_own],
+        two(2, width, block, block),
+        micros=1,
+    )
+    far_0, far_1 = exchanged(far_0, 0), got_far_1
+    out_high, out_low, part, ap_e1_high, ap_e1_low, group = call(
         mid_kernel,
-        [sent, full(rows, 2, block, block)]
-        + pair(half, deep)
-        + [full(rows, block, half)]
-        + pair(deep, half)
-        + [full(half, half)],
-        [tab, a01_high, a01_low, a23_high, a23_low, dinv, t0_high, t0_low, t_1, far_1, near_0],
-        two(2, width, block, block) + two(2, rows, block, half) + two(width, block, half),
-        micros=3,
-    )
-    near_1 = exchanged(near_1, 1)
-    far_0, far_1 = exchanged(far_0, 0), got_far_1
+        pair(half, deep) + [full(rows, block, half)] + pair(deep, half) + [full(half, half)],
+        [tab, a01_high, a01_low, a23_high, a23_low, far, near_0],
+        two(2, rows, block, half) + two(width, block, half),
+        micros=2,
+    )
     part_own, ap_e2_high, ap_e2_low, part_1 = call(
         same_kernel,
         [full(rows, block, half)] + pair(deep, half) + [full(half, 2 * half)],
-        [tab, a23_high, a23_low, out_high, out_low, far_0, group],
+        [tab, a23_high, a23_low, out_high, out_low, far_0, group, part_own],
         two(width, block, half),
         micros=1,
     )
     part_1 = exchanged(part_1, 1)
-    part_own, back_high, back_low = call(
-        own_part_kernel,
-        [full(rows, block, half)] + pair(width, block, block),
-        [tab, a01_high, a01_low, own, t, part_own],
-        two(rows, block, half),
-        micros=1,
-    )
     ap_own_high, ap_own_low, ap_o2_high, ap_o2_low, part_2 = call(
         second_kernel,
         pair(deep, half) * 2 + [full(half, 2 * half)],
@@ -531,12 +540,12 @@
     both_0 = exchanged(both_0, 0)
     (total,) = call(own_kernel, [full(half, 5 * half)], [own] + aps, two(half, deep), micros=2)
     out = []
-    for i, (offsets, got) in enumerate((((-3, -2, 2, 3), part_1), ((-1, 1), part_2), ((0,), part_3))):
+    for i, (offsets, got) in enumerate((((-3, -2), part_1), ((-1, 1, 2, 3), part_2), ((0,), part_3))):
         n = 2 * len(offsets)
         out = call(
             functools.partial(finish_kernel, offsets, PARTS_AT[i]),
             [full(2, 14, block, block)],
-            [coarse_inv, total, both_0, got, *out],
+            [coarse_inv, total] + ([both_0] if i else []) + [got, *out],
             [((n, 2, block, block), F32), pltpu.SemaphoreType.DMA((n,))],
             micros=1,
             in_hbm=(4,),

time: 63.1 us -> 59.8 us (0.948)
  waiting for transfers between devices: 12.5 us -> 10.6 us
  starting transfers between devices: 31.1 us -> 30 us
    ppermute x10, waiting for transfers between devices: 12.5 us -> 10.6 us  [exchanged(): return lax.ppermute(value, AXES, pairs)]
    ppermute x10, starting transfers between devices: 31.1 us -> 30 us  [exchanged(): return lax.ppermute(value, AXES, pairs)]
    pallas_call x13 -> x14, Pallas kernels: 18.7 us -> 18.8 us  [call(): pl.pallas_call(body, out_shape=outs, in_specs=specs(ins, in_hbm), out_spe...]
  transfers between devices with their start and end apart: 10 -> 10, of which waited for: 4 -> 5; matrix products, arithmetic and copies ran while one was open for 0% -> 0% of each run, Pallas kernels for 17% -> 20%
where the time goes in v1:
time: 59.8 us; the launch traced here: 59.7 us
  starting transfers between devices  30 us (50%)
  Pallas kernels  18.8 us (31%)
  waiting for transfers between devices  10.6 us (18%)
    ppermute x10, starting transfers between devices, exchanged(): return lax.ppermute(value, AXES, pairs)  30 us
    pallas_call x14, Pallas kernels, call(): pl.pallas_call(body, out_shape=outs, in_specs=specs(ins, in_hbm), out_spe...  18.8 us
    ppermute x10, waiting for transfers between devices, exchanged(): return lax.ppermute(value, AXES, pairs)  10.6 us
  transfers between devices with their start and end apart: 10, of which 5 were waited for; matrix products, arithmetic and copies ran while one was open for 0% of the time, Pallas kernels for 20%

profile of v1, /device:TPU:0, one launch (start us, length us, event | category | flops | bytes accessed | tf_op | source)
XLA Modules:
  0.0 59.7 jit_solution(6610978433672118262)
XLA Ops:
  0.0 1.5 %shard_map.64 = (s32[96,128]{1,0:T(8,128)S(1)}, f32[4,128,128]{2,1,0:T(8,128)S(1)}, f32[4,128,128]{2,1,0:T(8,128)S(1)}, f32[8,128,128]{2,1,0:T(8,128)S(1)}) custom-call(s32[4096]{0:T(1024)} %bitcast.5, s32[1024]{0:T(1024)} %agg_hbm.1, f32[8,128,128]{2,1,0:T(8,128)} %t_hbm.1), custom_call_target="tpu_custom_call" | custom-call | flops 3000000000 | bytes 1048576 | tf_op jit(solution)/shard_map/pallas_call | solution.py:438
  1.5 0.1 collective-permute-start
  1.6 8.9 %collective-permute-start.1 = (f32[4,128,128]{2,1,0:T(8,128)S(1)}, f32[4,128,128]{2,1,0:T(8,128)S(1)}, u32[]{:S(2)}, u32[]{:S(2)}) collective-permute-start(f32[4,128,128]{2,1,0:T(8,128)S(1)} %get-tuple-element.52), channel_id=1, source_target_pairs={{1,2},{2,1},{3,4},{4,3},{5,6},{6,5},{7,8},{8,7},{9,10},{10,9},{11,... | collective-permute-start | bytes 786440 | tf_op jit(solution)/shard_map/ppermute | solution.py:27
  10.5 1.3 %shard_map.65 = (f32[4,128,256]{2,1,0:T(8,128)S(1)}, f32[4,128,256]{2,1,0:T(8,128)S(1)}, f32[8,128,256]{2,1,0:T(8,128)S(1)}, bf16[2,8,128,128]{3,2,1,0:T(8,128)(...) custom-call(s32[96,128]{1,0:T(8,128)S(1)} %get-tuple-element.42.tab,, ...), custom_call_target="tpu_custom_call" | custom-call | flops 2000000000 | bytes 1048576 | tf_op jit(solution)/shard_map/pallas_call | solution.py:438
  11.7 0.1 collective-permute-start.2
  11.8 0.9 %collective-permute-start.3 = (f32[4,128,256]{2,1,0:T(8,128)S(1)}, f32[4,128,256]{2,1,0:T(8,128)S(1)}, u32[]{:S(2)}, u32[]{:S(2)}) collective-permute-start(f32[4,128,256]{2,1,0:T(8,128)S(1)} %get-tuple-element.62), channel_id=1, source_target_pairs={{1,2},{2,1},{3,4},{4,3},{5,6},{6,5},{7,8},{8,7},{9,10},{10,9},{11,... | collective-permute-start | bytes 1572872 | tf_op jit(solution)/shard_map/ppermute | solution.py:27
  12.8 0.7 %shard_map.67 = (f32[8,128,256]{2,1,0:T(8,128)S(1)}, bf16[4,128,128]{2,1,0:T(8,128)(2,1)S(1)}, bf16[4,128,128]{2,1,0:T(8,128)(2,1)S(1)}) custom-call(s32[96,128]{1,0:T(8,128)S(1)} %get-tuple-element.42.tab, bf16[8,128,256]{2,1,0:T(8,128)(2,1)S(1)} %get-tuple-element.45.a01_high, bf16[8,128,256]{2,1,0:T(8,128)(2,1)S(1)} %get-tuple-element.46.a01_low, ...), custom_call_target="tpu_custom_call" | custom-call | flops 1000000000 | bytes 1048576 | tf_op jit(solution)/shard_map/pallas_call | solution.py:438
  13.5 0.0 collective-permute-done.t_0
  13.5 0.5 shard_map.66
  14.0 0.5 collective-permute-done.1.t_1
  14.5 0.8 %shard_map.68 = (f32[4,2,128,128]{3,2,1,0:T(8,128)S(1)}, f32[8,2,128,128]{3,2,1,0:T(8,128)S(1)}) custom-call(s32[96,128]{1,0:T(8,128)S(1)} %get-tuple-element.42.tab, bf16[2,8,128,128]{3,2,1,0:T(8,128)(2,1)S(1)} %get-tuple-element.47.a_high, bf16[2,8,128,128]{3,2,1,0:T(8,128)(2,1)S(1)} %get-tuple-element.48.a_low, f32[8,128,128]{2,1,0:T(8,128)S(1)} %copy-done.1, ...), custom_call_target="tpu_custom_call" | custom-call | flops 1000000000 | bytes 1048576 | tf_op jit(solution)/shard_map/pallas_call | solution.py:438
  15.3 0.1 collective-permute-start.4
  15.4 7.3 %collective-permute-start.5 = (f32[4,2,128,128]{3,2,1,0:T(8,128)S(1)}, f32[4,2,128,128]{3,2,1,0:T(8,128)S(1)}, u32[]{:S(2)}, u32[]{:S(2)}) collective-permute-start(f32[4,2,128,128]{3,2,1,0:T(8,128)S(1)} %get-tuple-element.53.far_1), channel_id=1, source_target_pairs={{1,2},{2,1},{3,4},{4,3},{5,6},{6,5},{7,8},{8,7},{9,10},{10,9},{11,... | collective-permute-start | bytes 1572872 | tf_op jit(solution)/shard_map/ppermute | solution.py:27
  22.7 0.0 collective-permute-done.2.near_0
  22.7 2.2 %shard_map.69 = (bf16[256,1024]{1,0:T(8,128)(2,1)S(1)}, bf16[256,1024]{1,0:T(8,128)(2,1)S(1)}, f32[8,128,256]{2,1,0:T(8,128)S(1)}, bf16[1024,256]{1,0:T(8,128)(2...) custom-call(s32[96,128]{1,0:T(8,128)S(1)} %get-tuple-element.42.tab, ...), custom_call_target="tpu_custom_call" | custom-call | flops 2000000000 | bytes 1048576 | tf_op jit(solution)/shard_map/pallas_call | solution.py:438
  24.8 1.1 %collective-permute-done.3.near_1 = f32[4,128,256]{2,1,0:T(8,128)S(1)} collective-permute-done((f32[4,128,256]{2,1,0:T(8,128)S(1)}, f32[4,128,256]{2,1,0:T(8,128)S(1)}, u32[]{:S(2)}, u32[]{:S(2)}) %collective-permute-start.3) | collective-permute-done | bytes 524320 | tf_op jit(solution)/shard_map/ppermute | solution.py:27
  25.9 1.0 %shard_map.70 = (bf16[1024,256]{1,0:T(8,128)(2,1)S(1)}, bf16[1024,256]{1,0:T(8,128)(2,1)S(1)}, f32[256,256]{1,0:T(8,128)S(1)}) custom-call(s32[96,128]{1,0:T(8,128)S(1)} %get-tuple-element.42.tab, bf16[2,8,128,128]{3,2,1,0:T(8,128)(2,1)S(1)} %get-tuple-element.47.a_high, bf16[2,8,128,128]{3,2,1,0:T(8,128)(2,1)S(1)} %get-tuple-element.48.a_low, ...), custom_call_target="tpu_custom_call" | custom-call | flops 2000000000 | bytes 1048576 | tf_op jit(solution)/shard_map/pallas_call | solution.py:438
  27.0 1.1 %shard_map.71 = (f32[8,128,256]{2,1,0:T(8,128)S(1)}, bf16[1024,256]{1,0:T(8,128)(2,1)S(1)}, bf16[1024,256]{1,0:T(8,128)(2,1)S(1)}, f32[256,512]{1,0:T(8,128)S(1)}) custom-call(s32[96,128]{1,0:T(8,128)S(1)} %get-tuple-element.42.tab, bf16[2,8,128,128]{3,2,1,0:T(8,128)(2,1)S(1)} %get-tuple-element.47.a_high, ...), custom_call_target="tpu_custom_call" | custom-call | flops 1000000000 | bytes 1048576 | tf_op jit(solution)/shard_map/pallas_call | solution.py:438
  28.0 3.5 %collective-permute-done.5.far_1 = f32[4,2,128,128]{3,2,1,0:T(8,128)S(1)} collective-permute-done((f32[4,2,128,128]{3,2,1,0:T(8,128)S(1)}, f32[4,2,128,128]{3,2,1,0:T(8,128)S(1)}, u32[]{:S(2)}, u32[]{:S(2)}) %collective-permute-start.5) | collective-permute-done | bytes 524320 | tf_op jit(solution)/shard_map/ppermute | solution.py:27
  31.6 1.7 %shard_map.72 = (bf16[1024,256]{1,0:T(8,128)(2,1)S(1)}, bf16[1024,256]{1,0:T(8,128)(2,1)S(1)}, bf16[1024,256]{1,0:T(8,128)(2,1)S(1)}, bf16[1024,256]{1,0:T(8,128)(2,1)S(1)}, f32[256,512]{1,0:T(8,128)S(1)}) custom-call(s32[96,128]{1,0:T(8,128)S(1)} %get-tuple-element.42.tab, bf16[2,8,128,128]{3,2,1,0:T(8,128)(2,1)S(1)} %get-tuple-element.47.a_high, ...), custom_call_target="tpu_custom_call" | custom-call | flops 2000000000 | bytes 1048576 | tf_op jit(solution)/shard_map/pallas_call | solution.py:438
  33.2 2.5 %shard_map.74 = f32[256,1280]{1,0:T(8,128)S(1)} custom-call(s32[96,128]{1,0:T(8,128)S(1)} %get-tuple-element.42.tab, f32[8,2,128,128]{3,2,1,0:T(8,128)S(1)} %get-tuple-element.55.far, bf16[1024,256]{1,0:T(8,128)(2,1)S(1)} %get-tuple-element.57.refs_0_, bf16[1024,256]{1,0:T(8,128)(2,1)S(1)} %get-tuple-element.58.refs_1_, ...), custom_call_target="tpu_custom_call" | custom-call | flops 2000000000 | bytes 1048576 | tf_op jit(solution)/shard_map/pallas_call | solution.py:438
  35.7 0.3 collective-permute-start.6
  36.0 5.2 %collective-permute-start.9 = (f32[256,512]{1,0:T(8,128)S(1)}, f32[256,512]{1,0:T(8,128)S(1)}, u32[]{:S(2)}, u32[]{:S(2)}) collective-permute-start(f32[256,512]{1,0:T(8,128)S(1)} %get-tuple-element.78), channel_id=1, source_target_pairs={{1,2},{2,1},{3,4},{4,3},{5,6},{6,5},{7,8},{8,7},{9,10},{10,9},{11,... | collective-permute-start | bytes 1572872 | tf_op jit(solution)/shard_map/ppermute | solution.py:27
  41.2 2.0 %collective-permute-start.8 = (f32[256,512]{1,0:T(8,128)S(1)}, f32[256,512]{1,0:T(8,128)S(1)}, u32[]{:S(2)}, u32[]{:S(2)}) collective-permute-start(f32[256,512]{1,0:T(8,128)S(1)} %get-tuple-element.77), channel_id=1, source_target_pairs={{1,2},{2,1},{3,4},{4,3},{5,6},{6,5},{7,8},{8,7},{9,10},{10,9},{11,... | collective-permute-start | bytes 1572872 | tf_op jit(solution)/shard_map/ppermute | solution.py:27
  43.3 5.1 %collective-permute-start.7 = (f32[256,256]{1,0:T(8,128)S(1)}, f32[256,256]{1,0:T(8,128)S(1)}, u32[]{:S(2)}, u32[]{:S(2)}) collective-permute-start(f32[256,256]{1,0:T(8,128)S(1)} %get-tuple-element.76), channel_id=1, source_target_pairs={{1,2},{2,1},{3,4},{4,3},{5,6},{6,5},{7,8},{8,7},{9,10},{10,9},{11,... | collective-permute-start | bytes 786440 | tf_op jit(solution)/shard_map/ppermute | solution.py:27
  48.4 2.3 %shard_map.73.own = f32[256,1280]{1,0:T(8,128)S(1)} custom-call(f32[8,128,256]{2,1,0:T(8,128)S(1)} %get-tuple-element.44.own, bf16[1024,256]{1,0:T(8,128)(2,1)S(1)} %get-tuple-element.57.refs_0_, bf16[1024,256]{1,0:T(8,128)(2,1)S(1)} %get-tuple-element.58.refs_1_, bf16[1024,256]{1,0:T(8,128)(2,1)S(1)} %get-tuple-element.63.refs_2_, ...), custom_call_target="tpu_custom_call" | custom-call | flops 2000000000 | bytes 1048576 | tf_op jit(solution)/shard_map/pallas_call | solution.py:438
  50.7 1.1 %shard_map.75.refs_2_ = f32[2,14,128,128]{3,2,1,0:T(8,128)} custom-call(f32[2,128,128]{2,1,0:T(8,128)S(1)} %copy-done, f32[256,1280]{1,0:T(8,128)S(1)} %shard_map.73.own, f32[256,512]{1,0:T(8,128)S(1)} %collective-permute-done.9.refs_0_), custom_call_target="tpu_custom_call" | custom-call | flops 1000000000 | bytes 1048576 | tf_op jit(solution)/shard_map/pallas_call | solution.py:438
  51.8 4.0 %collective-permute-done.8.refs_1_ = f32[256,512]{1,0:T(8,128)S(1)} collective-permute-done((f32[256,512]{1,0:T(8,128)S(1)}, f32[256,512]{1,0:T(8,128)S(1)}, u32[]{:S(2)}, u32[]{:S(2)}) %collective-permute-start.8) | collective-permute-done | bytes 524320 | tf_op jit(solution)/shard_map/ppermute | solution.py:27
  55.8 0.0 collective-permute-done.6.refs_0_
  55.8 1.3 %shard_map.76.refs_2_ = f32[2,14,128,128]{3,2,1,0:T(8,128)} custom-call(f32[2,128,128]{2,1,0:T(8,128)S(1)} %copy-done, f32[256,1280]{1,0:T(8,128)S(1)} %shard_map.73.own, f32[256,1280]{1,0:T(8,128)S(1)} %collective-permute-done.6.refs_0_, f32[256,512]{1,0:T(8,128)S(1)} %collective-permute-done.8.refs_1_, ...), custom_call_target="tpu_custom_call", output_to_operand_aliasing={{}: (4, {})} | custom-call | flops 1000000000 | bytes 1048576 | tf_op jit(solution)/shard_map/pallas_call | solution.py:438
  57.0 1.5 %collective-permute-done.7.refs_1_ = f32[256,256]{1,0:T(8,128)S(1)} collective-permute-done((f32[256,256]{1,0:T(8,128)S(1)}, f32[256,256]{1,0:T(8,128)S(1)}, u32[]{:S(2)}, u32[]{:S(2)}) %collective-permute-start.7) | collective-permute-done | bytes 262176 | tf_op jit(solution)/shard_map/ppermute | solution.py:27
  58.6 1.0 %shard_map.77 = f32[2,14,128,128]{3,2,1,0:T(8,128)} custom-call(f32[2,128,128]{2,1,0:T(8,128)S(1)} %copy-done, f32[256,1280]{1,0:T(8,128)S(1)} %shard_map.73.own, f32[256,1280]{1,0:T(8,128)S(1)} %collective-permute-done.6.refs_0_, f32[256,256]{1,0:T(8,128)S(1)} %collective-permute-done.7.refs_1_, ...), custom_call_target="tpu_custom_call", output_to_operand_aliasing={{}: (4, {})} | custom-call | flops 1000000000 | bytes 1048576 | tf_op jit(solution)/shard_map/pallas_call | solution.py:438
  (8 shorter events, 0.0 us)
Async XLA Ops:
  0.0 10.5 %copy-start.1 = (f32[8,128,128]{2,1,0:T(8,128)S(1)}, f32[8,128,128]{2,1,0:T(8,128)}, u32[]{:S(2)}) copy-start(f32[8,128,128]{2,1,0:T(8,128)} %dinv.5) | copy-start | bytes 1572868
  0.0 10.5 %copy-start.2 = (f32[8,4,128,128]{3,2,1,0:T(8,128)S(1)}, f32[8,4,128,128]{3,2,1,0:T(8,128)}, u32[]{:S(2)}) copy-start(f32[8,4,128,128]{3,2,1,0:T(8,128)} %a.1) | copy-start | bytes 6291460
  1.5 12.0 %collective-permute-start = (f32[4,128,128]{2,1,0:T(8,128)S(1)}, f32[4,128,128]{2,1,0:T(8,128)S(1)}, u32[]{:S(2)}, u32[]{:S(2)}) collective-permute-start(f32[4,128,128]{2,1,0:T(8,128)S(1)} %get-tuple-element.49), channel_id=1, source_target_pairs={{0,1},{1,0},{2,3},{3,2},{4,5},{5,4},{6,7},{7,6},{8,9},{9,8},{10,11... | collective-permute-start | bytes 786440 | tf_op jit(solution)/shard_map/ppermute | solution.py:27
  1.6 12.9 %collective-permute-start.1 = (f32[4,128,128]{2,1,0:T(8,128)S(1)}, f32[4,128,128]{2,1,0:T(8,128)S(1)}, u32[]{:S(2)}, u32[]{:S(2)}) collective-permute-start(f32[4,128,128]{2,1,0:T(8,128)S(1)} %get-tuple-element.52), channel_id=1, source_target_pairs={{1,2},{2,1},{3,4},{4,3},{5,6},{6,5},{7,8},{8,7},{9,10},{10,9},{11,... | collective-permute-start | bytes 786440 | tf_op jit(solution)/shard_map/ppermute | solution.py:27
  11.7 10.9 %collective-permute-start.2 = (f32[4,128,256]{2,1,0:T(8,128)S(1)}, f32[4,128,256]{2,1,0:T(8,128)S(1)}, u32[]{:S(2)}, u32[]{:S(2)}) collective-permute-start(f32[4,128,256]{2,1,0:T(8,128)S(1)} %get-tuple-element.56), channel_id=1, source_target_pairs={{0,1},{1,0},{2,3},{3,2},{4,5},{5,4},{6,7},{7,6},{8,9},{9,8},{10,11... | collective-permute-start | bytes 1572872 | tf_op jit(solution)/shard_map/ppermute | solution.py:27
  11.8 14.1 %collective-permute-start.3 = (f32[4,128,256]{2,1,0:T(8,128)S(1)}, f32[4,128,256]{2,1,0:T(8,128)S(1)}, u32[]{:S(2)}, u32[]{:S(2)}) collective-permute-start(f32[4,128,256]{2,1,0:T(8,128)S(1)} %get-tuple-element.62), channel_id=1, source_target_pairs={{1,2},{2,1},{3,4},{4,3},{5,6},{6,5},{7,8},{8,7},{9,10},{10,9},{11,... | collective-permute-start | bytes 1572872 | tf_op jit(solution)/shard_map/ppermute | solution.py:27
  15.3 11.6 %collective-permute-start.4 = (f32[4,2,128,128]{3,2,1,0:T(8,128)S(1)}, f32[4,2,128,128]{3,2,1,0:T(8,128)S(1)}, u32[]{:S(2)}, u32[]{:S(2)}) collective-permute-start(f32[4,2,128,128]{3,2,1,0:T(8,128)S(1)} %get-tuple-element.65), channel_id=1, source_target_pairs={{0,1},{1,0},{2,3},{3,2},{4,5},{5,4},{6,7},{7,6},{8,9},{9,8},{10,11... | collective-permute-start | bytes 1572872 | tf_op jit(solution)/shard_map/ppermute | solution.py:27
  15.4 16.1 %collective-permute-start.5 = (f32[4,2,128,128]{3,2,1,0:T(8,128)S(1)}, f32[4,2,128,128]{3,2,1,0:T(8,128)S(1)}, u32[]{:S(2)}, u32[]{:S(2)}) collective-permute-start(f32[4,2,128,128]{3,2,1,0:T(8,128)S(1)} %get-tuple-element.53.far_1), channel_id=1, source_target_pairs={{1,2},{2,1},{3,4},{4,3},{5,6},{6,5},{7,8},{8,7},{9,10},{10,9},{11,... | collective-permute-start | bytes 1572872 | tf_op jit(solution)/shard_map/ppermute | solution.py:27
  35.7 20.0 %collective-permute-start.6 = (f32[256,1280]{1,0:T(8,128)S(1)}, f32[256,1280]{1,0:T(8,128)S(1)}, u32[]{:S(2)}, u32[]{:S(2)}) collective-permute-start(f32[256,1280]{1,0:T(8,128)S(1)} %shard_map.74), channel_id=1, source_target_pairs={{0,1},{1,0},{2,3},{3,2},{4,5},{5,4},{6,7},{7,6},{8,9},{9,8},{10,11... | collective-permute-start | bytes 3932168 | tf_op jit(solution)/shard_map/ppermute | solution.py:27
  36.0 14.7 %collective-permute-start.9 = (f32[256,512]{1,0:T(8,128)S(1)}, f32[256,512]{1,0:T(8,128)S(1)}, u32[]{:S(2)}, u32[]{:S(2)}) collective-permute-start(f32[256,512]{1,0:T(8,128)S(1)} %get-tuple-element.78), channel_id=1, source_target_pairs={{1,2},{2,1},{3,4},{4,3},{5,6},{6,5},{7,8},{8,7},{9,10},{10,9},{11,... | collective-permute-start | bytes 1572872 | tf_op jit(solution)/shard_map/ppermute | solution.py:27
  41.2 14.5 %collective-permute-start.8 = (f32[256,512]{1,0:T(8,128)S(1)}, f32[256,512]{1,0:T(8,128)S(1)}, u32[]{:S(2)}, u32[]{:S(2)}) collective-permute-start(f32[256,512]{1,0:T(8,128)S(1)} %get-tuple-element.77), channel_id=1, source_target_pairs={{1,2},{2,1},{3,4},{4,3},{5,6},{6,5},{7,8},{8,7},{9,10},{10,9},{11,... | collective-permute-start | bytes 1572872 | tf_op jit(solution)/shard_map/ppermute | solution.py:27
  43.3 7.4 %copy-start = (f32[2,128,128]{2,1,0:T(8,128)S(1)}, f32[2,128,128]{2,1,0:T(8,128)}, u32[]{:S(2)}) copy-start(f32[2,128,128]{2,1,0:T(8,128)} %inverse.5) | copy-start | bytes 393220
  43.3 15.3 %collective-permute-start.7 = (f32[256,256]{1,0:T(8,128)S(1)}, f32[256,256]{1,0:T(8,128)S(1)}, u32[]{:S(2)}, u32[]{:S(2)}) collective-permute-start(f32[256,256]{1,0:T(8,128)S(1)} %get-tuple-element.76), channel_id=1, source_target_pairs={{1,2},{2,1},{3,4},{4,3},{5,6},{6,5},{7,8},{8,7},{9,10},{10,9},{11,... | collective-permute-start | bytes 786440 | tf_op jit(solution)/shard_map/ppermute | solution.py:27

commit v2 on v1

--- a/solution.py
+++ b/solution.py
@@ -230,7 +230,7 @@
     return dot3(trans_high[...], trans_low[...], ap_high[...], ap_low[...])
 
 
-def far_kernel(tab, a_high, a_low, dinv, t0_high, t0_low, t_1, far_1, after, far_0, far, t_high, t_low):
+def far_kernel(tab, a_high, a_low, dinv, t0_high, t0_low, t_1, far_1, far_0, far, t_high, t_low):
     rows, block = far.shape[0], far.shape[2]
     width = rows // 2
     side = pair_side()
@@ -316,7 +316,7 @@
 
 
 def same_kernel(
-    tab, a_high, a_low, trans_high, trans_low, far_0, group, so_far,
+    tab, a_high, a_low, trans_high, trans_low, far_0, group,
     own_part, ap_high, ap_low, out_1,
     p_high, p_low,
 ):
@@ -329,11 +329,11 @@
         p_high[j, :, block:], p_low[j, :, block:] = split(far_0[j, side])
     here = far_columns(tab, side, a_high, a_low, p_high, p_low, ap_high, ap_low)
     for u, value in enumerate(here):
-        own_part[u] = so_far[u] + value
+        own_part[u] = value
     out_1[:, half:] = coarse_group(trans_high, trans_low, ap_high, ap_low)
 
 
-def own_part_kernel(tab, a01_high, a01_low, own, t, own_part, back_high, back_low, own_high, own_low):
+def own_part_kernel(tab, a01_high, a01_low, own, t, so_far, own_part, back_high, back_low, own_high, own_low):
     rows = own.shape[0]
     side = 1 - pair_side()
     for j in range(rows // 2):
@@ -342,7 +342,7 @@
         own_high[u], own_low[u] = split(own[u])
     for u in range(rows):
         near = entry(tab, NEAR + u)
-        own_part[u] = dot3(a01_high[u], a01_low[u], wide(own_high, u, near), wide(own_low, u, near))
+        own_part[u] = so_far[u] + dot3(a01_high[u], a01_low[u], wide(own_high, u, near), wide(own_low, u, near))
 
 
 def second_kernel(
@@ -486,17 +486,10 @@
     )
     got_far_1 = exchanged(far_1, 1)
     near_1 = exchanged(near_1, 1)
-    part_own, back_high, back_low = call(
-        own_part_kernel,
-        [full(rows, block, half)] + pair(width, block, block),
-        [tab, a01_high, a01_low, own, t],
-        two(rows, block, half),
-        micros=1,
-    )
     far_0, far = call(
         far_kernel,
         [sent, full(rows, 2, block, block)],
-        [tab, a23_high, a23_low, dinv, t0_high, t0_low, t_1, far_1, part_own],
+        [tab, a23_high, a23_low, dinv, t0_high, t0_low, t_1, far_1],
         two(2, width, block, block),
         micros=1,
     )
@@ -511,11 +504,18 @@
     part_own, ap_e2_high, ap_e2_low, part_1 = call(
         same_kernel,
         [full(rows, block, half)] + pair(deep, half) + [full(half, 2 * half)],
-        [tab, a23_high, a23_low, out_high, out_low, far_0, group, part_own],
+        [tab, a23_high, a23_low, out_high, out_low, far_0, group],
         two(width, block, half),
         micros=1,
     )
     part_1 = exchanged(part_1, 1)
+    part_own, back_high, back_low = call(
+        own_part_kernel,
+        [full(rows, block, half)] + pair(width, block, block),
+        [tab, a01_high, a01_low, own, t, part_own],
+        two(rows, block, half),
+        micros=1,
+    )
     ap_own_high, ap_own_low, ap_o2_high, ap_o2_low, part_2 = call(
         second_kernel,
         pair(deep, half) * 2 + [full(half, 2 * half)],

time: 59.8 us -> 60.9 us (1.018)
  transfers between devices with their start and end apart: 10 -> 10, of which waited for: 5 -> 4; matrix products, arithmetic and copies ran while one was open for 0% -> 0% of each run, Pallas kernels for 20% -> 20%
where the time goes in v2:
time: 60.9 us; the launch traced here: 60.8 us
  starting transfers between devices  30.6 us (50%)
  Pallas kernels  18.8 us (31%)
  waiting for transfers between devices  10.9 us (18%)
    ppermute x10, starting transfers between devices, exchanged(): return lax.ppermute(value, AXES, pairs)  30.6 us
    pallas_call x14, Pallas kernels, call(): pl.pallas_call(body, out_shape=outs, in_specs=specs(ins, in_hbm), out_spe...  18.8 us
    ppermute x10, waiting for transfers between devices, exchanged(): return lax.ppermute(value, AXES, pairs)  10.9 us
  transfers between devices with their start and end apart: 10, of which 4 were waited for; matrix products, arithmetic and copies ran while one was open for 0% of the time, Pallas kernels for 20%

profile of v2, /device:TPU:0, one launch (start us, length us, event | category | flops | bytes accessed | tf_op | source)
XLA Modules:
  0.0 60.8 jit_solution(15071511335127634448)
XLA Ops:
  0.0 1.5 %shard_map.64 = (s32[96,128]{1,0:T(8,128)S(1)}, f32[4,128,128]{2,1,0:T(8,128)S(1)}, f32[4,128,128]{2,1,0:T(8,128)S(1)}, f32[8,128,128]{2,1,0:T(8,128)S(1)}) custom-call(s32[4096]{0:T(1024)} %bitcast.5, s32[1024]{0:T(1024)} %agg_hbm.1, f32[8,128,128]{2,1,0:T(8,128)} %t_hbm.1), custom_call_target="tpu_custom_call" | custom-call | flops 3000000000 | bytes 1048576 | tf_op jit(solution)/shard_map/pallas_call | solution.py:438
  1.5 0.1 collective-permute-start
  1.6 0.2 copy-done.1
  1.7 0.1 copy-done.2
  1.8 1.2 %shard_map.65 = (f32[4,128,256]{2,1,0:T(8,128)S(1)}, f32[4,128,256]{2,1,0:T(8,128)S(1)}, f32[8,128,256]{2,1,0:T(8,128)S(1)}, bf16[2,8,128,128]{3,2,1,0:T(8,128)(...) custom-call(s32[96,128]{1,0:T(8,128)S(1)} %get-tuple-element.42.tab,, ...), custom_call_target="tpu_custom_call" | custom-call | flops 2000000000 | bytes 1048576 | tf_op jit(solution)/shard_map/pallas_call | solution.py:438
  3.1 0.3 collective-permute-start.2
  3.4 8.7 %collective-permute-start.1 = (f32[4,128,128]{2,1,0:T(8,128)S(1)}, f32[4,128,128]{2,1,0:T(8,128)S(1)}, u32[]{:S(2)}, u32[]{:S(2)}) collective-permute-start(f32[4,128,128]{2,1,0:T(8,128)S(1)} %get-tuple-element.52), channel_id=1, source_target_pairs={{1,2},{2,1},{3,4},{4,3},{5,6},{6,5},{7,8},{8,7},{9,10},{10,9},{11,... | collective-permute-start | bytes 786440 | tf_op jit(solution)/shard_map/ppermute | solution.py:27
  12.1 0.0 collective-permute-start.3
  12.1 0.0 collective-permute-done.t_0
  12.1 0.5 shard_map.66
  12.7 3.5 %collective-permute-done.1.t_1 = f32[4,128,128]{2,1,0:T(8,128)S(1)} collective-permute-done((f32[4,128,128]{2,1,0:T(8,128)S(1)}, f32[4,128,128]{2,1,0:T(8,128)S(1)}, u32[]{:S(2)}, u32[]{:S(2)}) %collective-permute-start.1) | collective-permute-done | bytes 262176 | tf_op jit(solution)/shard_map/ppermute | solution.py:27
  16.1 0.8 %shard_map.67 = (f32[4,2,128,128]{3,2,1,0:T(8,128)S(1)}, f32[8,2,128,128]{3,2,1,0:T(8,128)S(1)}) custom-call(s32[96,128]{1,0:T(8,128)S(1)} %get-tuple-element.42.tab, bf16[2,8,128,128]{3,2,1,0:T(8,128)(2,1)S(1)} %get-tuple-element.47.a_high, bf16[2,8,128,128]{3,2,1,0:T(8,128)(2,1)S(1)} %get-tuple-element.48.a_low, f32[8,128,128]{2,1,0:T(8,128)S(1)} %copy-done.2, ...), custom_call_target="tpu_custom_call" | custom-call | flops 1000000000 | bytes 1048576 | tf_op jit(solution)/shard_map/pallas_call | solution.py:438
  16.9 0.1 collective-permute-start.4
  17.0 7.3 %collective-permute-start.5 = (f32[4,2,128,128]{3,2,1,0:T(8,128)S(1)}, f32[4,2,128,128]{3,2,1,0:T(8,128)S(1)}, u32[]{:S(2)}, u32[]{:S(2)}) collective-permute-start(f32[4,2,128,128]{3,2,1,0:T(8,128)S(1)} %get-tuple-element.53.far_1), channel_id=1, source_target_pairs={{1,2},{2,1},{3,4},{4,3},{5,6},{6,5},{7,8},{8,7},{9,10},{10,9},{11,... | collective-permute-start | bytes 1572872 | tf_op jit(solution)/shard_map/ppermute | solution.py:27
  24.3 0.0 collective-permute-done.2.near_0
  24.3 2.2 %shard_map.68 = (bf16[256,1024]{1,0:T(8,128)(2,1)S(1)}, bf16[256,1024]{1,0:T(8,128)(2,1)S(1)}, f32[8,128,256]{2,1,0:T(8,128)S(1)}, bf16[1024,256]{1,0:T(8,128)(2...) custom-call(s32[96,128]{1,0:T(8,128)S(1)} %get-tuple-element.42.tab, ...), custom_call_target="tpu_custom_call" | custom-call | flops 2000000000 | bytes 1048576 | tf_op jit(solution)/shard_map/pallas_call | solution.py:438
  26.5 1.0 %shard_map.69 = (bf16[1024,256]{1,0:T(8,128)(2,1)S(1)}, bf16[1024,256]{1,0:T(8,128)(2,1)S(1)}, f32[256,256]{1,0:T(8,128)S(1)}) custom-call(s32[96,128]{1,0:T(8,128)S(1)} %get-tuple-element.42.tab, bf16[2,8,128,128]{3,2,1,0:T(8,128)(2,1)S(1)} %get-tuple-element.47.a_high, bf16[2,8,128,128]{3,2,1,0:T(8,128)(2,1)S(1)} %get-tuple-element.48.a_low, ...), custom_call_target="tpu_custom_call" | custom-call | flops 2000000000 | bytes 1048576 | tf_op jit(solution)/shard_map/pallas_call | solution.py:438
  27.5 1.1 %shard_map.70 = (f32[8,128,256]{2,1,0:T(8,128)S(1)}, bf16[1024,256]{1,0:T(8,128)(2,1)S(1)}, bf16[1024,256]{1,0:T(8,128)(2,1)S(1)}, f32[256,512]{1,0:T(8,128)S(1)}) custom-call(s32[96,128]{1,0:T(8,128)S(1)} %get-tuple-element.42.tab, bf16[2,8,128,128]{3,2,1,0:T(8,128)(2,1)S(1)} %get-tuple-element.47.a_high, ...), custom_call_target="tpu_custom_call" | custom-call | flops 1000000000 | bytes 1048576 | tf_op jit(solution)/shard_map/pallas_call | solution.py:438
  28.6 0.8 %shard_map.71 = (f32[8,128,256]{2,1,0:T(8,128)S(1)}, bf16[4,128,128]{2,1,0:T(8,128)(2,1)S(1)}, bf16[4,128,128]{2,1,0:T(8,128)(2,1)S(1)}) custom-call(s32[96,128]{1,0:T(8,128)S(1)} %get-tuple-element.42.tab, bf16[8,128,256]{2,1,0:T(8,128)(2,1)S(1)} %get-tuple-element.45.a01_high, bf16[8,128,256]{2,1,0:T(8,128)(2,1)S(1)} %get-tuple-element.46.a01_low, ...), custom_call_target="tpu_custom_call" | custom-call | flops 1000000000 | bytes 1048576 | tf_op jit(solution)/shard_map/pallas_call | solution.py:438
  29.3 2.4 %collective-permute-done.5.far_1 = f32[4,2,128,128]{3,2,1,0:T(8,128)S(1)} collective-permute-done((f32[4,2,128,128]{3,2,1,0:T(8,128)S(1)}, f32[4,2,128,128]{3,2,1,0:T(8,128)S(1)}, u32[]{:S(2)}, u32[]{:S(2)}) %collective-permute-start.5) | collective-permute-done | bytes 524320 | tf_op jit(solution)/shard_map/ppermute | solution.py:27
  31.7 1.7 %shard_map.72 = (bf16[1024,256]{1,0:T(8,128)(2,1)S(1)}, bf16[1024,256]{1,0:T(8,128)(2,1)S(1)}, bf16[1024,256]{1,0:T(8,128)(2,1)S(1)}, bf16[1024,256]{1,0:T(8,128)(2,1)S(1)}, f32[256,512]{1,0:T(8,128)S(1)}) custom-call(s32[96,128]{1,0:T(8,128)S(1)} %get-tuple-element.42.tab, bf16[2,8,128,128]{3,2,1,0:T(8,128)(2,1)S(1)} %get-tuple-element.47.a_high, ...), custom_call_target="tpu_custom_call" | custom-call | flops 2000000000 | bytes 1048576 | tf_op jit(solution)/shard_map/pallas_call | solution.py:438
  33.4 2.5 %shard_map.74 = f32[256,1280]{1,0:T(8,128)S(1)} custom-call(s32[96,128]{1,0:T(8,128)S(1)} %get-tuple-element.42.tab, f32[8,2,128,128]{3,2,1,0:T(8,128)S(1)} %get-tuple-element.54.far, bf16[1024,256]{1,0:T(8,128)(2,1)S(1)} %get-tuple-element.56.refs_0_, bf16[1024,256]{1,0:T(8,128)(2,1)S(1)} %get-tuple-element.57.refs_1_, ...), custom_call_target="tpu_custom_call" | custom-call | flops 2000000000 | bytes 1048576 | tf_op jit(solution)/shard_map/pallas_call | solution.py:438
  35.9 0.3 collective-permute-start.6
  36.2 6.7 %collective-permute-start.9 = (f32[256,512]{1,0:T(8,128)S(1)}, f32[256,512]{1,0:T(8,128)S(1)}, u32[]{:S(2)}, u32[]{:S(2)}) collective-permute-start(f32[256,512]{1,0:T(8,128)S(1)} %get-tuple-element.78), channel_id=1, source_target_pairs={{1,2},{2,1},{3,4},{4,3},{5,6},{6,5},{7,8},{8,7},{9,10},{10,9},{11,... | collective-permute-start | bytes 1572872 | tf_op jit(solution)/shard_map/ppermute | solution.py:27
  42.9 0.6 collective-permute-start.8
  43.5 6.6 %collective-permute-start.7 = (f32[256,256]{1,0:T(8,128)S(1)}, f32[256,256]{1,0:T(8,128)S(1)}, u32[]{:S(2)}, u32[]{:S(2)}) collective-permute-start(f32[256,256]{1,0:T(8,128)S(1)} %get-tuple-element.76), channel_id=1, source_target_pairs={{1,2},{2,1},{3,4},{4,3},{5,6},{6,5},{7,8},{8,7},{9,10},{10,9},{11,... | collective-permute-start | bytes 786440 | tf_op jit(solution)/shard_map/ppermute | solution.py:27
  50.0 2.3 %shard_map.73.own = f32[256,1280]{1,0:T(8,128)S(1)} custom-call(f32[8,128,256]{2,1,0:T(8,128)S(1)} %get-tuple-element.44.own, bf16[1024,256]{1,0:T(8,128)(2,1)S(1)} %get-tuple-element.56.refs_0_, bf16[1024,256]{1,0:T(8,128)(2,1)S(1)} %get-tuple-element.57.refs_1_, bf16[1024,256]{1,0:T(8,128)(2,1)S(1)} %get-tuple-element.62.refs_2_, ...), custom_call_target="tpu_custom_call" | custom-call | flops 2000000000 | bytes 1048576 | tf_op jit(solution)/shard_map/pallas_call | solution.py:438
  52.3 1.1 %shard_map.75.refs_2_ = f32[2,14,128,128]{3,2,1,0:T(8,128)} custom-call(f32[2,128,128]{2,1,0:T(8,128)S(1)} %copy-done, f32[256,1280]{1,0:T(8,128)S(1)} %shard_map.73.own, f32[256,512]{1,0:T(8,128)S(1)} %collective-permute-done.9.refs_0_), custom_call_target="tpu_custom_call" | custom-call | flops 1000000000 | bytes 1048576 | tf_op jit(solution)/shard_map/pallas_call | solution.py:438
  53.4 3.5 %collective-permute-done.8.refs_1_ = f32[256,512]{1,0:T(8,128)S(1)} collective-permute-done((f32[256,512]{1,0:T(8,128)S(1)}, f32[256,512]{1,0:T(8,128)S(1)}, u32[]{:S(2)}, u32[]{:S(2)}) %collective-permute-start.8) | collective-permute-done | bytes 524320 | tf_op jit(solution)/shard_map/ppermute | solution.py:27
  56.9 1.3 %shard_map.76.refs_2_ = f32[2,14,128,128]{3,2,1,0:T(8,128)} custom-call(f32[2,128,128]{2,1,0:T(8,128)S(1)} %copy-done, f32[256,1280]{1,0:T(8,128)S(1)} %shard_map.73.own, f32[256,1280]{1,0:T(8,128)S(1)} %collective-permute-done.6.refs_0_, f32[256,512]{1,0:T(8,128)S(1)} %collective-permute-done.8.refs_1_, ...), custom_call_target="tpu_custom_call", output_to_operand_aliasing={{}: (4, {})} | custom-call | flops 1000000000 | bytes 1048576 | tf_op jit(solution)/shard_map/pallas_call | solution.py:438
  58.2 1.5 %collective-permute-done.7.refs_1_ = f32[256,256]{1,0:T(8,128)S(1)} collective-permute-done((f32[256,256]{1,0:T(8,128)S(1)}, f32[256,256]{1,0:T(8,128)S(1)}, u32[]{:S(2)}, u32[]{:S(2)}) %collective-permute-start.7) | collective-permute-done | bytes 262176 | tf_op jit(solution)/shard_map/ppermute | solution.py:27
  59.7 1.0 %shard_map.77 = f32[2,14,128,128]{3,2,1,0:T(8,128)} custom-call(f32[2,128,128]{2,1,0:T(8,128)S(1)} %copy-done, f32[256,1280]{1,0:T(8,128)S(1)} %shard_map.73.own, f32[256,1280]{1,0:T(8,128)S(1)} %collective-permute-done.6.refs_0_, f32[256,256]{1,0:T(8,128)S(1)} %collective-permute-done.7.refs_1_, ...), custom_call_target="tpu_custom_call", output_to_operand_aliasing={{}: (4, {})} | custom-call | flops 1000000000 | bytes 1048576 | tf_op jit(solution)/shard_map/pallas_call | solution.py:438
  (8 shorter events, 0.0 us)
Async XLA Ops:
  0.0 1.7 %copy-start.1 = (f32[8,4,128,128]{3,2,1,0:T(8,128)S(1)}, f32[8,4,128,128]{3,2,1,0:T(8,128)}, u32[]{:S(2)}) copy-start(f32[8,4,128,128]{3,2,1,0:T(8,128)} %a.1) | copy-start | bytes 6291460
  0.0 1.8 %copy-start.2 = (f32[8,128,128]{2,1,0:T(8,128)S(1)}, f32[8,128,128]{2,1,0:T(8,128)}, u32[]{:S(2)}) copy-start(f32[8,128,128]{2,1,0:T(8,128)} %dinv.5) | copy-start | bytes 1572868
  1.5 10.6 %collective-permute-start = (f32[4,128,128]{2,1,0:T(8,128)S(1)}, f32[4,128,128]{2,1,0:T(8,128)S(1)}, u32[]{:S(2)}, u32[]{:S(2)}) collective-permute-start(f32[4,128,128]{2,1,0:T(8,128)S(1)} %get-tuple-element.49), channel_id=1, source_target_pairs={{0,1},{1,0},{2,3},{3,2},{4,5},{5,4},{6,7},{7,6},{8,9},{9,8},{10,11... | collective-permute-start | bytes 786440 | tf_op jit(solution)/shard_map/ppermute | solution.py:27
  3.1 21.2 %collective-permute-start.2 = (f32[4,128,256]{2,1,0:T(8,128)S(1)}, f32[4,128,256]{2,1,0:T(8,128)S(1)}, u32[]{:S(2)}, u32[]{:S(2)}) collective-permute-start(f32[4,128,256]{2,1,0:T(8,128)S(1)} %get-tuple-element.55), channel_id=1, source_target_pairs={{0,1},{1,0},{2,3},{3,2},{4,5},{5,4},{6,7},{7,6},{8,9},{9,8},{10,11... | collective-permute-start | bytes 1572872 | tf_op jit(solution)/shard_map/ppermute | solution.py:27
  3.4 12.7 %collective-permute-start.1 = (f32[4,128,128]{2,1,0:T(8,128)S(1)}, f32[4,128,128]{2,1,0:T(8,128)S(1)}, u32[]{:S(2)}, u32[]{:S(2)}) collective-permute-start(f32[4,128,128]{2,1,0:T(8,128)S(1)} %get-tuple-element.52), channel_id=1, source_target_pairs={{1,2},{2,1},{3,4},{4,3},{5,6},{6,5},{7,8},{8,7},{9,10},{10,9},{11,... | collective-permute-start | bytes 786440 | tf_op jit(solution)/shard_map/ppermute | solution.py:27
  12.1 14.4 %collective-permute-start.3 = (f32[4,128,256]{2,1,0:T(8,128)S(1)}, f32[4,128,256]{2,1,0:T(8,128)S(1)}, u32[]{:S(2)}, u32[]{:S(2)}) collective-permute-start(f32[4,128,256]{2,1,0:T(8,128)S(1)} %get-tuple-element.61), channel_id=1, source_target_pairs={{1,2},{2,1},{3,4},{4,3},{5,6},{6,5},{7,8},{8,7},{9,10},{10,9},{11,... | collective-permute-start | bytes 1572872 | tf_op jit(solution)/shard_map/ppermute | solution.py:27
  16.9 10.5 %collective-permute-start.4 = (f32[4,2,128,128]{3,2,1,0:T(8,128)S(1)}, f32[4,2,128,128]{3,2,1,0:T(8,128)S(1)}, u32[]{:S(2)}, u32[]{:S(2)}) collective-permute-start(f32[4,2,128,128]{3,2,1,0:T(8,128)S(1)} %get-tuple-element.64), channel_id=1, source_target_pairs={{0,1},{1,0},{2,3},{3,2},{4,5},{5,4},{6,7},{7,6},{8,9},{9,8},{10,11... | collective-permute-start | bytes 1572872 | tf_op jit(solution)/shard_map/ppermute | solution.py:27
  17.0 14.7 %collective-permute-start.5 = (f32[4,2,128,128]{3,2,1,0:T(8,128)S(1)}, f32[4,2,128,128]{3,2,1,0:T(8,128)S(1)}, u32[]{:S(2)}, u32[]{:S(2)}) collective-permute-start(f32[4,2,128,128]{3,2,1,0:T(8,128)S(1)} %get-tuple-element.53.far_1), channel_id=1, source_target_pairs={{1,2},{2,1},{3,4},{4,3},{5,6},{6,5},{7,8},{8,7},{9,10},{10,9},{11,... | collective-permute-start | bytes 1572872 | tf_op jit(solution)/shard_map/ppermute | solution.py:27
  35.9 21.0 %collective-permute-start.6 = (f32[256,1280]{1,0:T(8,128)S(1)}, f32[256,1280]{1,0:T(8,128)S(1)}, u32[]{:S(2)}, u32[]{:S(2)}) collective-permute-start(f32[256,1280]{1,0:T(8,128)S(1)} %shard_map.74), channel_id=1, source_target_pairs={{0,1},{1,0},{2,3},{3,2},{4,5},{5,4},{6,7},{7,6},{8,9},{9,8},{10,11... | collective-permute-start | bytes 3932168 | tf_op jit(solution)/shard_map/ppermute | solution.py:27
  36.2 16.1 %collective-permute-start.9 = (f32[256,512]{1,0:T(8,128)S(1)}, f32[256,512]{1,0:T(8,128)S(1)}, u32[]{:S(2)}, u32[]{:S(2)}) collective-permute-start(f32[256,512]{1,0:T(8,128)S(1)} %get-tuple-element.78), channel_id=1, source_target_pairs={{1,2},{2,1},{3,4},{4,3},{5,6},{6,5},{7,8},{8,7},{9,10},{10,9},{11,... | collective-permute-start | bytes 1572872 | tf_op jit(solution)/shard_map/ppermute | solution.py:27
  42.9 14.0 %collective-permute-start.8 = (f32[256,512]{1,0:T(8,128)S(1)}, f32[256,512]{1,0:T(8,128)S(1)}, u32[]{:S(2)}, u32[]{:S(2)}) collective-permute-start(f32[256,512]{1,0:T(8,128)S(1)} %get-tuple-element.77), channel_id=1, source_target_pairs={{1,2},{2,1},{3,4},{4,3},{5,6},{6,5},{7,8},{8,7},{9,10},{10,9},{11,... | collective-permute-start | bytes 1572872 | tf_op jit(solution)/shard_map/ppermute | solution.py:27
  43.5 8.9 %copy-start = (f32[2,128,128]{2,1,0:T(8,128)S(1)}, f32[2,128,128]{2,1,0:T(8,128)}, u32[]{:S(2)}) copy-start(f32[2,128,128]{2,1,0:T(8,128)} %inverse.5) | copy-start | bytes 393220
  43.5 16.2 %collective-permute-start.7 = (f32[256,256]{1,0:T(8,128)S(1)}, f32[256,256]{1,0:T(8,128)S(1)}, u32[]{:S(2)}, u32[]{:S(2)}) collective-permute-start(f32[256,256]{1,0:T(8,128)S(1)} %get-tuple-element.76), channel_id=1, source_target_pairs={{1,2},{2,1},{3,4},{4,3},{5,6},{6,5},{7,8},{8,7},{9,10},{10,9},{11,... | collective-permute-start | bytes 786440 | tf_op jit(solution)/shard_map/ppermute | solution.py:27

commit v3 on v2

--- a/solution.py
+++ b/solution.py
@@ -57,7 +57,20 @@
     return tab[pl.ds(i, 1), :][0, 0]
 
 
-def load_kernel(devices, cols_hbm, agg_hbm, t_hbm, tab, t_0, t_1, t, cols, agg, rank, sem):
+def far_partner():
+    return lax.axis_index("gy") == 0
+
+
+def load_kernel(
+    devices, cols_hbm, agg_hbm, t_hbm, dinv_hbm, a_hbm,
+    tab, t_0, t_1, t, near_0, near_1, own, a_high, a_low, a01_high, a01_low,
+    cols, agg, rank, dinv, a, sem,
+):
+    early = [
+        pltpu.make_async_copy(dinv_hbm, dinv, sem.at[5]),
+        pltpu.make_async_copy(a_hbm, a, sem.at[6]),
+    ]
+
     rows, width = t.shape[0], t.shape[0] // 2
     device = lax.axis_index("gx") * lax.axis_size("gy") + lax.axis_index("gy")
     previous = lax.rem(device + devices - 1, devices)
@@ -125,6 +138,14 @@
         for k in range(4):
             note(tab, OWN_LAB + 4 * u + k, agg[col(2, row, k)])
 
+    @pl.when(far_partner())
+    def _():
+        for copy in early:
+            copy.start()
+        for copy in early:
+            copy.wait()
+        near_blocks(tab, a, t, dinv, near_0, near_1, own, a_high, a_low, a01_high, a01_low)
+
 
 def put(value, label, column):
     return jnp.where(label == column, value, jnp.zeros_like(value))
@@ -158,7 +179,7 @@
     return jnp.concatenate([ref[place] for place in places], axis=0)
 
 
-def near_kernel(tab, a, t, dinv, near_0, near_1, own, a_high, a_low, a01_high, a01_low):
+def near_blocks(tab, a, t, dinv, near_0, near_1, own, a_high, a_low, a01_high, a01_low):
     rows, width = own.shape[0], near_1.shape[0]
     for u, value in enumerate(near_tiles(tab, a, t, dinv, range(rows))):
         own[u] = value
@@ -171,6 +192,10 @@
         a01_high[u], a01_low[u] = split(jnp.concatenate([a[row, 0], a[row, 1]], axis=1))
         for which in (BELOW, ABOVE):
             a_high[which, u], a_low[which, u] = split(a[row, 2 + which])
+
+
+def near_kernel(tab, a, t, dinv, *refs):
+    pl.when(jnp.logical_not(far_partner()))(lambda: near_blocks(tab, a, t, dinv, *refs[7:]))
 
 
 def far_blocks(tab, a_high, a_low, dinv, t_high, t_low, order):
@@ -458,26 +483,26 @@
     tile = full(width, block, half)
     cols = a_cols.reshape(-1, ROW_CHUNK, 4).transpose(0, 2, 1).reshape(-1)
 
-    tab, t_0, t_1, t = call(
+    near_shapes = [tile, tile, full(rows, block, half)] + pair(2, rows, block, block) + pair(rows, block, half)
+    tab, t_0, t_1, t, *near = call(
         functools.partial(load_kernel, devices),
-        [shape((TAB, LANES), jnp.int32)] + [full(width, block, block)] * 2 + [full(*t_blocks.shape)],
-        [pltpu.with_memory_space_constraint(x, pltpu.HBM) for x in (cols, t_agg, t_blocks)],
+        [shape((TAB, LANES), jnp.int32)] + [full(width, block, block)] * 2 + [full(*t_blocks.shape)] + near_shapes,
+        [pltpu.with_memory_space_constraint(x, pltpu.HBM) for x in (cols, t_agg, t_blocks, dinv, a)],
         [
             pltpu.SMEM((3 * 4 * ROW_CHUNK,), jnp.int32),
             pltpu.SMEM(t_agg.shape, jnp.int32),
             pltpu.SMEM((8 * rows,), jnp.int32),
-            pltpu.SemaphoreType.DMA((5,)),
+            (dinv.shape, F32),
+            (a.shape, F32),
+            pltpu.SemaphoreType.DMA((7,)),
         ],
         micros=3,
-        in_hbm=(0, 1, 2),
-    )
+        in_hbm=(0, 1, 2, 3, 4),
+    )
+    t_0 = exchanged(t_0, 0)
     t_1 = exchanged(t_1, 1)
-    t_0 = exchanged(t_0, 0)
     near_0, near_1, own, a23_high, a23_low, a01_high, a01_low = call(
-        near_kernel,
-        [tile, tile, full(rows, block, half)] + pair(2, rows, block, block) + pair(rows, block, half),
-        [tab, a, t, dinv],
-        micros=2,
+        near_kernel, near_shapes, [tab, a, t, dinv, *near], micros=2, aliases={4 + i: i for i in range(7)}
     )
     near_0 = exchanged(near_0, 0)
     sent = full(width, 2, block, block)

time: 60.9 us -> 61 us (level)
  starting transfers between devices: 30.6 us -> 28 us
  Pallas kernels: 18.8 us -> 20.6 us
  waiting for transfers between devices: 10.9 us -> 11.9 us
    ppermute x10, starting transfers between devices: 30.6 us -> 28 us  [exchanged(): return lax.ppermute(value, AXES, pairs)]
    pallas_call x14, Pallas kernels: 18.8 us -> 20.6 us  [call(): pl.pallas_call(body, out_shape=outs, in_specs=specs(ins, in_hbm), out_spe...]
    ppermute x10, waiting for transfers between devices: 10.9 us -> 11.9 us  [exchanged(): return lax.ppermute(value, AXES, pairs)]
  transfers between devices with their start and end apart: 10 -> 10, of which waited for: 4 -> 4; matrix products, arithmetic and copies ran while one was open for 0% -> 0% of each run, Pallas kernels for 20% -> 18%
where the time goes in v3:
time: 61 us; the launch traced here: 60.8 us
  starting transfers between devices  28 us (46%)
  Pallas kernels  20.6 us (34%)
  waiting for transfers between devices  11.9 us (20%)
    ppermute x10, starting transfers between devices, exchanged(): return lax.ppermute(value, AXES, pairs)  28 us
    pallas_call x14, Pallas kernels, call(): pl.pallas_call(body, out_shape=outs, in_specs=specs(ins, in_hbm), out_spe...  20.6 us
    ppermute x10, waiting for transfers between devices, exchanged(): return lax.ppermute(value, AXES, pairs)  11.9 us
  transfers between devices with their start and end apart: 10, of which 4 were waited for; matrix products, arithmetic and copies ran while one was open for 0% of the time, Pallas kernels for 18%

profile of v3, /device:TPU:0, one launch (start us, length us, event | category | flops | bytes accessed | tf_op | source)
XLA Modules:
  0.0 60.8 jit_solution(4918364536498971820)
XLA Ops:
  0.0 4.5 %shard_map.64 = (s32[96,128]{1,0:T(8,128)S(1)}, f32[4,128,128]{2,1,0:T(8,128)S(1)}, f32[4,128,128]{2,1,0:T(8,128)S(1)}, f32[8,128,128]{2,1,0:T(8,128)S(1)}, f32[...) custom-call(s32[4096]{0:T(1024)} %bitcast.5, ...), custom_call_target="tpu_custom_call" | custom-call | flops 3000000000 | bytes 1048576 | tf_op jit(solution)/shard_map/pallas_call | solution.py:463
  4.5 0.1 collective-permute-start
  4.7 1.8 %collective-permute-start.2 = (f32[4,128,256]{2,1,0:T(8,128)S(1)}, f32[4,128,256]{2,1,0:T(8,128)S(1)}, u32[]{:S(2)}, u32[]{:S(2)}) collective-permute-start(f32[4,128,256]{2,1,0:T(8,128)S(1)} %get-tuple-element.69), channel_id=1, source_target_pairs={{0,1},{1,0},{2,3},{3,2},{4,5},{5,4},{6,7},{7,6},{8,9},{9,8},{10,11... | collective-permute-start | bytes 1572872 | tf_op jit(solution)/shard_map/ppermute | solution.py:27
  6.5 5.6 %collective-permute-start.1 = (f32[4,128,128]{2,1,0:T(8,128)S(1)}, f32[4,128,128]{2,1,0:T(8,128)S(1)}, u32[]{:S(2)}, u32[]{:S(2)}) collective-permute-start(f32[4,128,128]{2,1,0:T(8,128)S(1)} %get-tuple-element.66), channel_id=1, source_target_pairs={{1,2},{2,1},{3,4},{4,3},{5,6},{6,5},{7,8},{8,7},{9,10},{10,9},{11,... | collective-permute-start | bytes 786440 | tf_op jit(solution)/shard_map/ppermute | solution.py:27
  12.1 1.6 %collective-permute-start.3 = (f32[4,128,256]{2,1,0:T(8,128)S(1)}, f32[4,128,256]{2,1,0:T(8,128)S(1)}, u32[]{:S(2)}, u32[]{:S(2)}) collective-permute-start(f32[4,128,256]{2,1,0:T(8,128)S(1)} %get-tuple-element.75), channel_id=1, source_target_pairs={{1,2},{2,1},{3,4},{4,3},{5,6},{6,5},{7,8},{8,7},{9,10},{10,9},{11,... | collective-permute-start | bytes 1572872 | tf_op jit(solution)/shard_map/ppermute | solution.py:27
  13.6 0.0 collective-permute-done.t_0
  13.6 0.5 shard_map.66
  14.2 3.5 %collective-permute-done.1.t_1 = f32[4,128,128]{2,1,0:T(8,128)S(1)} collective-permute-done((f32[4,128,128]{2,1,0:T(8,128)S(1)}, f32[4,128,128]{2,1,0:T(8,128)S(1)}, u32[]{:S(2)}, u32[]{:S(2)}) %collective-permute-start.1) | collective-permute-done | bytes 262176 | tf_op jit(solution)/shard_map/ppermute | solution.py:27
  17.7 0.8 %shard_map.67 = (f32[4,2,128,128]{3,2,1,0:T(8,128)S(1)}, f32[8,2,128,128]{3,2,1,0:T(8,128)S(1)}) custom-call(s32[96,128]{1,0:T(8,128)S(1)} %get-tuple-element.49.tab, bf16[2,8,128,128]{3,2,1,0:T(8,128)(2,1)S(1)} %get-tuple-element.61.a_high, bf16[2,8,128,128]{3,2,1,0:T(8,128)(2,1)S(1)} %get-tuple-element.62.a_low, f32[8,128,128]{2,1,0:T(8,128)S(1)} %copy-done.2, ...), custom_call_target="tpu_custom_call" | custom-call | flops 1000000000 | bytes 1048576 | tf_op jit(solution)/shard_map/pallas_call | solution.py:463
  18.5 0.1 collective-permute-start.4
  18.6 5.9 %collective-permute-start.5 = (f32[4,2,128,128]{3,2,1,0:T(8,128)S(1)}, f32[4,2,128,128]{3,2,1,0:T(8,128)S(1)}, u32[]{:S(2)}, u32[]{:S(2)}) collective-permute-start(f32[4,2,128,128]{3,2,1,0:T(8,128)S(1)} %get-tuple-element.67.far_1), channel_id=1, source_target_pairs={{1,2},{2,1},{3,4},{4,3},{5,6},{6,5},{7,8},{8,7},{9,10},{10,9},{11,... | collective-permute-start | bytes 1572872 | tf_op jit(solution)/shard_map/ppermute | solution.py:27
  24.5 0.0 collective-permute-done.2.near_0
  24.5 2.2 %shard_map.68 = (bf16[256,1024]{1,0:T(8,128)(2,1)S(1)}, bf16[256,1024]{1,0:T(8,128)(2,1)S(1)}, f32[8,128,256]{2,1,0:T(8,128)S(1)}, bf16[1024,256]{1,0:T(8,128)(2...) custom-call(s32[96,128]{1,0:T(8,128)S(1)} %get-tuple-element.49.tab, ...), custom_call_target="tpu_custom_call" | custom-call | flops 2000000000 | bytes 1048576 | tf_op jit(solution)/shard_map/pallas_call | solution.py:463
  26.6 0.0 collective-permute-done.3.near_1
  26.6 1.0 %shard_map.69 = (bf16[1024,256]{1,0:T(8,128)(2,1)S(1)}, bf16[1024,256]{1,0:T(8,128)(2,1)S(1)}, f32[256,256]{1,0:T(8,128)S(1)}) custom-call(s32[96,128]{1,0:T(8,128)S(1)} %get-tuple-element.49.tab, bf16[2,8,128,128]{3,2,1,0:T(8,128)(2,1)S(1)} %get-tuple-element.61.a_high, bf16[2,8,128,128]{3,2,1,0:T(8,128)(2,1)S(1)} %get-tuple-element.62.a_low, ...), custom_call_target="tpu_custom_call" | custom-call | flops 2000000000 | bytes 1048576 | tf_op jit(solution)/shard_map/pallas_call | solution.py:463
  27.6 0.0 collective-permute-done.4.far_0
  27.7 1.1 %shard_map.70 = (f32[8,128,256]{2,1,0:T(8,128)S(1)}, bf16[1024,256]{1,0:T(8,128)(2,1)S(1)}, bf16[1024,256]{1,0:T(8,128)(2,1)S(1)}, f32[256,512]{1,0:T(8,128)S(1)}) custom-call(s32[96,128]{1,0:T(8,128)S(1)} %get-tuple-element.49.tab, bf16[2,8,128,128]{3,2,1,0:T(8,128)(2,1)S(1)} %get-tuple-element.61.a_high, ...), custom_call_target="tpu_custom_call" | custom-call | flops 1000000000 | bytes 1048576 | tf_op jit(solution)/shard_map/pallas_call | solution.py:463
  28.7 0.8 %shard_map.71 = (f32[8,128,256]{2,1,0:T(8,128)S(1)}, bf16[4,128,128]{2,1,0:T(8,128)(2,1)S(1)}, bf16[4,128,128]{2,1,0:T(8,128)(2,1)S(1)}) custom-call(s32[96,128]{1,0:T(8,128)S(1)} %get-tuple-element.49.tab, bf16[8,128,256]{2,1,0:T(8,128)(2,1)S(1)} %get-tuple-element.59.a01_high, bf16[8,128,256]{2,1,0:T(8,128)(2,1)S(1)} %get-tuple-element.60.a01_low, ...), custom_call_target="tpu_custom_call" | custom-call | flops 1000000000 | bytes 1048576 | tf_op jit(solution)/shard_map/pallas_call | solution.py:463
  29.5 3.4 %collective-permute-done.5.far_1 = f32[4,2,128,128]{3,2,1,0:T(8,128)S(1)} collective-permute-done((f32[4,2,128,128]{3,2,1,0:T(8,128)S(1)}, f32[4,2,128,128]{3,2,1,0:T(8,128)S(1)}, u32[]{:S(2)}, u32[]{:S(2)}) %collective-permute-start.5) | collective-permute-done | bytes 524320 | tf_op jit(solution)/shard_map/ppermute | solution.py:27
  32.9 1.7 %shard_map.72 = (bf16[1024,256]{1,0:T(8,128)(2,1)S(1)}, bf16[1024,256]{1,0:T(8,128)(2,1)S(1)}, bf16[1024,256]{1,0:T(8,128)(2,1)S(1)}, bf16[1024,256]{1,0:T(8,128)(2,1)S(1)}, f32[256,512]{1,0:T(8,128)S(1)}) custom-call(s32[96,128]{1,0:T(8,128)S(1)} %get-tuple-element.49.tab, bf16[2,8,128,128]{3,2,1,0:T(8,128)(2,1)S(1)} %get-tuple-element.61.a_high, ...), custom_call_target="tpu_custom_call" | custom-call | flops 2000000000 | bytes 1048576 | tf_op jit(solution)/shard_map/pallas_call | solution.py:463
  34.6 2.5 %shard_map.74 = f32[256,1280]{1,0:T(8,128)S(1)} custom-call(s32[96,128]{1,0:T(8,128)S(1)} %get-tuple-element.49.tab, f32[8,2,128,128]{3,2,1,0:T(8,128)S(1)} %get-tuple-element.68.far, bf16[1024,256]{1,0:T(8,128)(2,1)S(1)} %get-tuple-element.70.refs_0_, bf16[1024,256]{1,0:T(8,128)(2,1)S(1)} %get-tuple-element.71.refs_1_, ...), custom_call_target="tpu_custom_call" | custom-call | flops 2000000000 | bytes 1048576 | tf_op jit(solution)/shard_map/pallas_call | solution.py:463
  37.1 0.1 collective-permute-start.6
  37.2 5.7 %collective-permute-start.9 = (f32[256,512]{1,0:T(8,128)S(1)}, f32[256,512]{1,0:T(8,128)S(1)}, u32[]{:S(2)}, u32[]{:S(2)}) collective-permute-start(f32[256,512]{1,0:T(8,128)S(1)} %get-tuple-element.92), channel_id=1, source_target_pairs={{1,2},{2,1},{3,4},{4,3},{5,6},{6,5},{7,8},{8,7},{9,10},{10,9},{11,... | collective-permute-start | bytes 1572872 | tf_op jit(solution)/shard_map/ppermute | solution.py:27
  42.9 1.6 %collective-permute-start.8 = (f32[256,512]{1,0:T(8,128)S(1)}, f32[256,512]{1,0:T(8,128)S(1)}, u32[]{:S(2)}, u32[]{:S(2)}) collective-permute-start(f32[256,512]{1,0:T(8,128)S(1)} %get-tuple-element.91), channel_id=1, source_target_pairs={{1,2},{2,1},{3,4},{4,3},{5,6},{6,5},{7,8},{8,7},{9,10},{10,9},{11,... | collective-permute-start | bytes 1572872 | tf_op jit(solution)/shard_map/ppermute | solution.py:27
  44.4 5.6 %collective-permute-start.7 = (f32[256,256]{1,0:T(8,128)S(1)}, f32[256,256]{1,0:T(8,128)S(1)}, u32[]{:S(2)}, u32[]{:S(2)}) collective-permute-start(f32[256,256]{1,0:T(8,128)S(1)} %get-tuple-element.90), channel_id=1, source_target_pairs={{1,2},{2,1},{3,4},{4,3},{5,6},{6,5},{7,8},{8,7},{9,10},{10,9},{11,... | collective-permute-start | bytes 786440 | tf_op jit(solution)/shard_map/ppermute | solution.py:27
  50.0 2.3 %shard_map.73.own = f32[256,1280]{1,0:T(8,128)S(1)} custom-call(f32[8,128,256]{2,1,0:T(8,128)S(1)} %get-tuple-element.58.own, bf16[1024,256]{1,0:T(8,128)(2,1)S(1)} %get-tuple-element.70.refs_0_, bf16[1024,256]{1,0:T(8,128)(2,1)S(1)} %get-tuple-element.71.refs_1_, bf16[1024,256]{1,0:T(8,128)(2,1)S(1)} %get-tuple-element.76.refs_2_, ...), custom_call_target="tpu_custom_call" | custom-call | flops 2000000000 | bytes 1048576 | tf_op jit(solution)/shard_map/pallas_call | solution.py:463
  52.3 0.0 collective-permute-done.9.refs_0_
  52.3 1.1 %shard_map.75.refs_2_ = f32[2,14,128,128]{3,2,1,0:T(8,128)} custom-call(f32[2,128,128]{2,1,0:T(8,128)S(1)} %copy-done, f32[256,1280]{1,0:T(8,128)S(1)} %shard_map.73.own, f32[256,512]{1,0:T(8,128)S(1)} %collective-permute-done.9.refs_0_), custom_call_target="tpu_custom_call" | custom-call | flops 1000000000 | bytes 1048576 | tf_op jit(solution)/shard_map/pallas_call | solution.py:463
  53.4 3.5 %collective-permute-done.8.refs_1_ = f32[256,512]{1,0:T(8,128)S(1)} collective-permute-done((f32[256,512]{1,0:T(8,128)S(1)}, f32[256,512]{1,0:T(8,128)S(1)}, u32[]{:S(2)}, u32[]{:S(2)}) %collective-permute-start.8) | collective-permute-done | bytes 524320 | tf_op jit(solution)/shard_map/ppermute | solution.py:27
  56.9 1.3 %shard_map.76.refs_2_ = f32[2,14,128,128]{3,2,1,0:T(8,128)} custom-call(f32[2,128,128]{2,1,0:T(8,128)S(1)} %copy-done, f32[256,1280]{1,0:T(8,128)S(1)} %shard_map.73.own, f32[256,1280]{1,0:T(8,128)S(1)} %collective-permute-done.6.refs_0_, f32[256,512]{1,0:T(8,128)S(1)} %collective-permute-done.8.refs_1_, ...), custom_call_target="tpu_custom_call", output_to_operand_aliasing={{}: (4, {})} | custom-call | flops 1000000000 | bytes 1048576 | tf_op jit(solution)/shard_map/pallas_call | solution.py:463
  58.2 1.5 %collective-permute-done.7.refs_1_ = f32[256,256]{1,0:T(8,128)S(1)} collective-permute-done((f32[256,256]{1,0:T(8,128)S(1)}, f32[256,256]{1,0:T(8,128)S(1)}, u32[]{:S(2)}, u32[]{:S(2)}) %collective-permute-start.7) | collective-permute-done | bytes 262176 | tf_op jit(solution)/shard_map/ppermute | solution.py:27
  59.7 1.0 %shard_map.77 = f32[2,14,128,128]{3,2,1,0:T(8,128)} custom-call(f32[2,128,128]{2,1,0:T(8,128)S(1)} %copy-done, f32[256,1280]{1,0:T(8,128)S(1)} %shard_map.73.own, f32[256,1280]{1,0:T(8,128)S(1)} %collective-permute-done.6.refs_0_, f32[256,256]{1,0:T(8,128)S(1)} %collective-permute-done.7.refs_1_, ...), custom_call_target="tpu_custom_call", output_to_operand_aliasing={{}: (4, {})} | custom-call | flops 1000000000 | bytes 1048576 | tf_op jit(solution)/shard_map/pallas_call | solution.py:463
  (8 shorter events, 0.0 us)
Async XLA Ops:
  0.0 4.6 %copy-start.1 = (f32[8,4,128,128]{3,2,1,0:T(8,128)S(1)}, f32[8,4,128,128]{3,2,1,0:T(8,128)}, u32[]{:S(2)}) copy-start(f32[8,4,128,128]{3,2,1,0:T(8,128)} %a.1) | copy-start | bytes 6291460
  0.0 4.6 %copy-start.2 = (f32[8,128,128]{2,1,0:T(8,128)S(1)}, f32[8,128,128]{2,1,0:T(8,128)}, u32[]{:S(2)}) copy-start(f32[8,128,128]{2,1,0:T(8,128)} %dinv.5) | copy-start | bytes 1572868
  4.5 9.1 %collective-permute-start = (f32[4,128,128]{2,1,0:T(8,128)S(1)}, f32[4,128,128]{2,1,0:T(8,128)S(1)}, u32[]{:S(2)}, u32[]{:S(2)}) collective-permute-start(f32[4,128,128]{2,1,0:T(8,128)S(1)} %get-tuple-element.63), channel_id=1, source_target_pairs={{0,1},{1,0},{2,3},{3,2},{4,5},{5,4},{6,7},{7,6},{8,9},{9,8},{10,11... | collective-permute-start | bytes 786440 | tf_op jit(solution)/shard_map/ppermute | solution.py:27
  4.7 19.8 %collective-permute-start.2 = (f32[4,128,256]{2,1,0:T(8,128)S(1)}, f32[4,128,256]{2,1,0:T(8,128)S(1)}, u32[]{:S(2)}, u32[]{:S(2)}) collective-permute-start(f32[4,128,256]{2,1,0:T(8,128)S(1)} %get-tuple-element.69), channel_id=1, source_target_pairs={{0,1},{1,0},{2,3},{3,2},{4,5},{5,4},{6,7},{7,6},{8,9},{9,8},{10,11... | collective-permute-start | bytes 1572872 | tf_op jit(solution)/shard_map/ppermute | solution.py:27
  6.5 11.2 %collective-permute-start.1 = (f32[4,128,128]{2,1,0:T(8,128)S(1)}, f32[4,128,128]{2,1,0:T(8,128)S(1)}, u32[]{:S(2)}, u32[]{:S(2)}) collective-permute-start(f32[4,128,128]{2,1,0:T(8,128)S(1)} %get-tuple-element.66), channel_id=1, source_target_pairs={{1,2},{2,1},{3,4},{4,3},{5,6},{6,5},{7,8},{8,7},{9,10},{10,9},{11,... | collective-permute-start | bytes 786440 | tf_op jit(solution)/shard_map/ppermute | solution.py:27
  12.1 14.5 %collective-permute-start.3 = (f32[4,128,256]{2,1,0:T(8,128)S(1)}, f32[4,128,256]{2,1,0:T(8,128)S(1)}, u32[]{:S(2)}, u32[]{:S(2)}) collective-permute-start(f32[4,128,256]{2,1,0:T(8,128)S(1)} %get-tuple-element.75), channel_id=1, source_target_pairs={{1,2},{2,1},{3,4},{4,3},{5,6},{6,5},{7,8},{8,7},{9,10},{10,9},{11,... | collective-permute-start | bytes 1572872 | tf_op jit(solution)/shard_map/ppermute | solution.py:27
  18.5 9.2 %collective-permute-start.4 = (f32[4,2,128,128]{3,2,1,0:T(8,128)S(1)}, f32[4,2,128,128]{3,2,1,0:T(8,128)S(1)}, u32[]{:S(2)}, u32[]{:S(2)}) collective-permute-start(f32[4,2,128,128]{3,2,1,0:T(8,128)S(1)} %get-tuple-element.78), channel_id=1, source_target_pairs={{0,1},{1,0},{2,3},{3,2},{4,5},{5,4},{6,7},{7,6},{8,9},{9,8},{10,11... | collective-permute-start | bytes 1572872 | tf_op jit(solution)/shard_map/ppermute | solution.py:27
  18.6 14.3 %collective-permute-start.5 = (f32[4,2,128,128]{3,2,1,0:T(8,128)S(1)}, f32[4,2,128,128]{3,2,1,0:T(8,128)S(1)}, u32[]{:S(2)}, u32[]{:S(2)}) collective-permute-start(f32[4,2,128,128]{3,2,1,0:T(8,128)S(1)} %get-tuple-element.67.far_1), channel_id=1, source_target_pairs={{1,2},{2,1},{3,4},{4,3},{5,6},{6,5},{7,8},{8,7},{9,10},{10,9},{11,... | collective-permute-start | bytes 1572872 | tf_op jit(solution)/shard_map/ppermute | solution.py:27
  37.1 19.8 %collective-permute-start.6 = (f32[256,1280]{1,0:T(8,128)S(1)}, f32[256,1280]{1,0:T(8,128)S(1)}, u32[]{:S(2)}, u32[]{:S(2)}) collective-permute-start(f32[256,1280]{1,0:T(8,128)S(1)} %shard_map.74), channel_id=1, source_target_pairs={{0,1},{1,0},{2,3},{3,2},{4,5},{5,4},{6,7},{7,6},{8,9},{9,8},{10,11... | collective-permute-start | bytes 3932168 | tf_op jit(solution)/shard_map/ppermute | solution.py:27
  37.2 15.2 %collective-permute-start.9 = (f32[256,512]{1,0:T(8,128)S(1)}, f32[256,512]{1,0:T(8,128)S(1)}, u32[]{:S(2)}, u32[]{:S(2)}) collective-permute-start(f32[256,512]{1,0:T(8,128)S(1)} %get-tuple-element.92), channel_id=1, source_target_pairs={{1,2},{2,1},{3,4},{4,3},{5,6},{6,5},{7,8},{8,7},{9,10},{10,9},{11,... | collective-permute-start | bytes 1572872 | tf_op jit(solution)/shard_map/ppermute | solution.py:27
  42.9 14.0 %collective-permute-start.8 = (f32[256,512]{1,0:T(8,128)S(1)}, f32[256,512]{1,0:T(8,128)S(1)}, u32[]{:S(2)}, u32[]{:S(2)}) collective-permute-start(f32[256,512]{1,0:T(8,128)S(1)} %get-tuple-element.91), channel_id=1, source_target_pairs={{1,2},{2,1},{3,4},{4,3},{5,6},{6,5},{7,8},{8,7},{9,10},{10,9},{11,... | collective-permute-start | bytes 1572872 | tf_op jit(solution)/shard_map/ppermute | solution.py:27
  44.4 7.9 %copy-start = (f32[2,128,128]{2,1,0:T(8,128)S(1)}, f32[2,128,128]{2,1,0:T(8,128)}, u32[]{:S(2)}) copy-start(f32[2,128,128]{2,1,0:T(8,128)} %inverse.5) | copy-start | bytes 393220
  44.4 15.3 %collective-permute-start.7 = (f32[256,256]{1,0:T(8,128)S(1)}, f32[256,256]{1,0:T(8,128)S(1)}, u32[]{:S(2)}, u32[]{:S(2)}) collective-permute-start(f32[256,256]{1,0:T(8,128)S(1)} %get-tuple-element.90), channel_id=1, source_target_pairs={{1,2},{2,1},{3,4},{4,3},{5,6},{6,5},{7,8},{8,7},{9,10},{10,9},{11,... | collective-permute-start | bytes 786440 | tf_op jit(solution)/shard_map/ppermute | solution.py:27
